TPU v7x, 256 devices: a 2x2x32 block of a 4x8x32 slice. The times are simulated.
256 devices in a mesh: groups: 4 (over x, y), dp: 64 (over z, core).
Axes of the slice: x: 2, y: 2, z: 32, core: 2. Of those that a mesh axis runs over, the one named last changes fastest.
The devices are a block of a 4x8x32 slice.
Arguments:
- tokens: bfloat16 [98304, 8192], P(('groups', 'dp')), parts along dimension 0, may hold values from -6 to 6
- base_weight: bfloat16 [8192, 768], P('dp'), may hold values from -0.0625 to 0.0625
- down_stack: bfloat16 [8192, 512], P('dp'), may hold values from -0.0625 to 0.0625
- up_stack: bfloat16 [512, 768], replicated, may hold values from -0.75 to 0.75
- adapter_scale: float32 [8], replicated, may hold values from 0.5 to 2
- lengths: int32 [512], P(('groups', 'dp')), parts along dimension 0, may hold values from 1 to 256, as said below
- adapter_ids: int32 [512], P(('groups', 'dp')), parts along dimension 0, may hold values from 0 to 7
Outputs:
- projected: bfloat16 [98304, 768], P(('groups', 'dp')), parts along dimension 0
There are 4 independent parts, one for each index of `groups`. A program takes and returns all parts, laid end to end along the dimension named above; an argument that names none is the same for every part. Nothing has to cross between parts.
Inputs may be any that keep to these rules, and one draw needn't show every extreme that they name: `lengths`: each index of dp holds two requests whose block counts ceil(length / 128) add up to exactly 3.
All inputs are finite; a program needn't handle non-finite values.
Results may differ from a plain program's by a relative error of at most 0.0042.
Values may be sent and summed in bfloat16 or wider, within the bound.
No kernel may reach another device: no remote copies, remote signals or barrier semaphores. Data moves between devices by JAX's collectives and lax.ppermute only.
A program may use at most 128 MiB of HBM per device.

v0:
```python
import jax
import jax.numpy as jnp
from jax import lax
from jax.experimental import pallas as pl
from jax.experimental.pallas import tpu as pltpu
from jax.sharding import PartitionSpec as P

RANK = 64
BLOCK = 128
CORES = 2
TILE = 256

VMEM = pl.BlockSpec(memory_space=pltpu.VMEM)
SMEM = pl.BlockSpec(memory_space=pltpu.SMEM)
ANY = pl.BlockSpec(memory_space=pl.ANY)
LIMIT = 20 * 2**20


def side_by_side_kernel(left_ref, right_ref, whole_ref, top_ref, low_ref, sem):
    half, cut = top_ref.shape[0], left_ref.shape[1]
    copies = []
    for ref, rows in ((top_ref, slice(0, half)), (low_ref, slice(half, 2 * half)), (whole_ref, slice(0, 2 * half))):
        for source, columns in ((left_ref, slice(0, cut)), (right_ref, slice(cut, whole_ref.shape[1]))):
            copies.append(
                pltpu.make_async_copy(source.at[rows, :], ref.at[:, columns], sem.at[len(copies)])
            )
    for copy in copies:
        copy.start()
    for copy in copies:
        copy.wait()


def side_by_side(left, right):
    rows, width = left.shape[0], left.shape[1] + right.shape[1]
    whole = jax.ShapeDtypeStruct((rows, width), left.dtype)
    half = jax.ShapeDtypeStruct((rows // 2, width), left.dtype)
    return pl.pallas_call(
        side_by_side_kernel,
        out_shape=[whole, half, half],
        in_specs=[pl.BlockSpec(memory_space=pltpu.HBM)] * 2,
        out_specs=[VMEM] * 3,
        scratch_shapes=[pltpu.SemaphoreType.DMA((6,))],
        compiler_params=pltpu.CompilerParams(vmem_limit_bytes=LIMIT),
    )(left, right)


def stack_kernel(*refs):
    rows = refs[0].shape[0]
    for k, ref in enumerate(refs[:-1]):
        refs[-1][k * rows : (k + 1) * rows, :] = ref[...]


def stack(pieces):
    rows, width = pieces[0].shape
    return pl.pallas_call(
        stack_kernel,
        out_shape=jax.ShapeDtypeStruct((rows * len(pieces), width), pieces[0].dtype),
        in_specs=[VMEM] * len(pieces),
        out_specs=VMEM,
        compiler_params=pltpu.CompilerParams(vmem_limit_bytes=LIMIT),
        cost_estimate=pl.CostEstimate(flops=2**20, bytes_accessed=4 * rows * width * len(pieces), transcendentals=0),
    )(*pieces)


def accumulate_kernel(sources, part_count, first, chips, where_ref, tokens_ref, *refs):
    parts = refs[:part_count]
    acc_in = None if first else refs[part_count]
    out_ref, tok, sem = refs[part_count + (0 if first else 1) :]
    chip, sign, core = where_ref[0], where_ref[1], where_ref[2]
    copies = []
    for k, (distance, mine) in enumerate(sources):
        source = lax.rem(chip + sign * distance + chips, chips)
        side = lax.rem(core + distance + (0 if mine else 1), CORES)
        column = (source * CORES + side) * BLOCK
        copies.append(
            pltpu.make_async_copy(
                tokens_ref.at[:, pl.ds(pl.multiple_of(column, BLOCK), BLOCK)],
                tok.at[:, k * BLOCK : (k + 1) * BLOCK],
                sem.at[k],
            )
        )
    for copy in copies:
        copy.start()
    for copy in copies:
        copy.wait()

    def column_tile(k, carry):
        at = pl.ds(pl.multiple_of(k * TILE, TILE), TILE)
        total = None if first else acc_in[:, at]
        begin = 0
        for part in parts:
            end = begin + part.shape[0]
            term = jnp.dot(tok[:, begin:end], part[:, at], preferred_element_type=jnp.float32)
            total = term if total is None else total + term
            begin = end
        out_ref[:, at] = total.astype(out_ref.dtype)
        return carry

    lax.fori_loop(0, out_ref.shape[1] // TILE, column_tile, 0)


def accumulate(acc, tokens, where, chips, sources, parts, dtype=jnp.float32):
    rows, width = tokens.shape[0], parts[0].shape[1]
    first = acc is None
    n = len(sources)
    return pl.pallas_call(
        lambda *refs: accumulate_kernel(sources, len(parts), first, chips, *refs),
        out_shape=jax.ShapeDtypeStruct((rows, width), dtype),
        in_specs=[SMEM, ANY] + [VMEM] * (len(parts) + (0 if first else 1)),
        out_specs=VMEM,
        input_output_aliases={} if first or dtype != acc.dtype else {2 + len(parts): 0},
        scratch_shapes=[pltpu.VMEM((rows, n * BLOCK), jnp.bfloat16), pltpu.SemaphoreType.DMA((n,))],
        compiler_params=pltpu.CompilerParams(vmem_limit_bytes=LIMIT),
        cost_estimate=pl.CostEstimate(
            flops=2 * rows * n * BLOCK * width,
            bytes_accessed=2 * n * BLOCK * (rows + width) + 8 * rows * width,
            transcendentals=0,
        ),
    )(where, tokens, *parts, *([] if first else [acc]))


def finish_kernel(lengths_ref, ids_ref, scale_ref, acc_ref, got_ref, up_ref, out_ref):
    rows, cols = out_ref.shape
    deep = up_ref.shape[0]
    boundary = (lengths_ref[0] + BLOCK - 1) // BLOCK * BLOCK
    position = lax.broadcasted_iota(jnp.int32, (rows, 1), 0)
    second = position >= boundary
    offset = jnp.where(second, position - boundary, position)
    live = offset < jnp.where(second, lengths_ref[1], lengths_ref[0])
    adapter = jnp.where(second, ids_ref[1], ids_ref[0])
    scale = jnp.where(second, scale_ref[ids_ref[1]], scale_ref[ids_ref[0]])
    low = (acc_ref[:, cols:] + got_ref[:, cols:].astype(jnp.float32)).astype(jnp.bfloat16)
    owner = lax.broadcasted_iota(jnp.int32, (rows, deep), 1) // RANK
    wide = jnp.where(owner == adapter, low, jnp.zeros((), jnp.bfloat16))
    for k in range(cols // TILE):
        at = slice(k * TILE, (k + 1) * TILE)
        extra = jnp.dot(wide, up_ref[:, at], preferred_element_type=jnp.float32)
        base = acc_ref[:, at] + got_ref[:, at].astype(jnp.float32)
        out_ref[:, at] = jnp.where(live, base + scale * extra, 0.0).astype(out_ref.dtype)


def finish(acc, got, up, scale, lengths, ids):
    rows, width = acc.shape
    deep, cols = up.shape
    return pl.pallas_call(
        finish_kernel,
        out_shape=jax.ShapeDtypeStruct((rows, cols), jnp.bfloat16),
        in_specs=[SMEM, SMEM, SMEM, VMEM, VMEM, VMEM],
        out_specs=VMEM,
        compiler_params=pltpu.CompilerParams(vmem_limit_bytes=LIMIT),
        cost_estimate=pl.CostEstimate(flops=2 * rows * deep * cols, bytes_accessed=8 * rows * width, transcendentals=0),
    )(lengths, ids, scale, acc, got, up)


BATCHES = ((1, 2), (3, 5), (6, 8), (9, 10), (11, 12), (13, 14), (15, 15))
GROUPS = ((0,), (1,), (2,), (3, 4), (5, 6))


def solution(mesh):
    dp = mesh.shape["dp"]
    groups = mesh.shape["groups"]
    chips = dp // CORES
    far = chips // 2
    first_x = [d.coords[0] for d in mesh.devices[:, 0]]
    per_x = first_x.count(first_x[0])

    def parity(g):
        return (g // per_x + g % per_x) % 2

    def flat(g, z, c):
        return g * dp + z % chips * CORES + c

    places = [(g, z, c) for g in range(groups) for z in range(chips) for c in range(CORES)]
    forth = {(g, z, c): c == (parity(g) + z) % CORES for g, z, c in places}
    along = [(flat(*p), flat(p[0], p[1] + (1 if forth[p] else -1), 1 - p[2])) for p in places]
    across = [(flat(*p), flat(p[0] ^ per_x if forth[p] else p[0] ^ 1, p[1], 1 - p[2])) for p in places]
    mate = [(i, i ^ 1) for i in range(dp)]
    both = ("groups", "dp")

    def local(tokens, base_weight, down_stack, up_stack, adapter_scale, lengths, adapter_ids):
        place = lax.axis_index("dp")
        group = lax.axis_index("groups")
        chip, core = place // CORES, place % CORES
        sign = jnp.where(core == (parity(group) + chip) % CORES, -1, 1)
        where = jnp.stack([chip, sign, core]).astype(jnp.int32)
        own, a, b = side_by_side(base_weight, down_stack)
        theirs = lax.ppermute(tokens, "dp", mate)
        pieces = {}
        for s in range(1, far + 1):
            a = lax.ppermute(a, both, along)
            b = lax.ppermute(b, both, along)
            pieces[s] = [a, b]
        acc = acc_theirs = None
        for k, batches in enumerate(GROUPS):
            parts, sources = [], []
            for batch in batches:
                steps = range(BATCHES[batch][0], BATCHES[batch][1] + 1)
                near = stack([p for s in steps for p in pieces[s]])
                got = lax.ppermute(near, both, across)
                mine = [(s, True) for s in steps]
                if batch == len(BATCHES) - 1:
                    near = stack([p for s in (*steps, far) for p in pieces[s]])
                    mine.append((far, True))
                parts += [near, got]
                sources += mine + [(s, False) for s in steps]
            if k == 0:
                parts, sources = parts + [own], sources + [(0, True)]
            acc_theirs = accumulate(acc_theirs, theirs, where, chips, sources, parts)
            acc = accumulate(acc, tokens, where, chips, sources, parts)
        rest = lax.ppermute(acc_theirs, "dp", mate)
        return finish(acc, rest, up_stack, adapter_scale, lengths, adapter_ids)

    in_specs = (
        P(("groups", "dp"), None),
        P("dp", None),
        P("dp", None),
        P(),
        P(),
        P(("groups", "dp")),
        P(("groups", "dp")),
    )
    return jax.shard_map(local, mesh=mesh, in_specs=in_specs, out_specs=P(("groups", "dp"), None), check_vma=False)
```

profile of v0, /device:TPU:37, one launch (start us, length us, event | category | flops | bytes accessed | tf_op | source)
XLA Modules:
  0.0 169.9 jit_solution(11707472884404911911)
XLA Ops:
  0.0 20.4 %collective-permute-start.39 = (bf16[384,8192]{1,0:T(8,128)(2,1)}, bf16[384,8192]{1,0:T(8,128)(2,1)}, u32[]{:S(2)}, u32[]{:S(2)}) collective-permute-start(bf16[384,8192]{1,0:T(8,128)(2,1)} %refs_1_.9), channel_id=1, source_target_pairs={{0,1},{1,0},{2,3},{3,2},{4,5},{5,4},{6,7},{7,6},{8,9},{9,8},{10,11... | collective-permute-start | bytes 18874376 | tf_op jit(solution)/shard_map/ppermute | solution.py:187
  23.1 3.7 %collective-permute-start = (bf16[64,1280]{1,0:T(8,128)(2,1)S(1)}, bf16[64,1280]{1,0:T(8,128)(2,1)S(1)}, u32[]{:S(2)}, u32[]{:S(2)}) collective-permute-start(bf16[64,1280]{1,0:T(8,128)(2,1)S(1)} %get-tuple-element.8), channel_id=1, source_target_pairs={{0,3},{1,62},{2,1},{3,4},{4,7},{5,2},{6,5},{7,8},{8,11},{9,6},{10,... | collective-permute-start | bytes 491528 | tf_op jit(solution)/shard_map/ppermute | solution.py:190
  29.0 3.7 %collective-permute-start.1 = (bf16[64,1280]{1,0:T(8,128)(2,1)S(1)}, bf16[64,1280]{1,0:T(8,128)(2,1)S(1)}, u32[]{:S(2)}, u32[]{:S(2)}) collective-permute-start(bf16[64,1280]{1,0:T(8,128)(2,1)S(1)} %collective-permute-done.refs_0_), channel_id=1, source_target_pairs={{0,3},{1,62},{2,1},{3,4},{4,7},{5,2},{6,5},{7,8},{8,11},{9,6},{10,... | collective-permute-start | bytes 491528 | tf_op jit(solution)/shard_map/ppermute | solution.py:190
  35.0 3.7 %collective-permute-start.2 = (bf16[64,1280]{1,0:T(8,128)(2,1)S(1)}, bf16[64,1280]{1,0:T(8,128)(2,1)S(1)}, u32[]{:S(2)}, u32[]{:S(2)}) collective-permute-start(bf16[64,1280]{1,0:T(8,128)(2,1)S(1)} %collective-permute-done.1.refs_2_), channel_id=1, source_target_pairs={{0,3},{1,62},{2,1},{3,4},{4,7},{5,2},{6,5},{7,8},{8,11},{9,6},{10,... | collective-permute-start | bytes 491528 | tf_op jit(solution)/shard_map/ppermute | solution.py:190
  40.9 3.7 %collective-permute-start.3 = (bf16[64,1280]{1,0:T(8,128)(2,1)S(1)}, bf16[64,1280]{1,0:T(8,128)(2,1)S(1)}, u32[]{:S(2)}, u32[]{:S(2)}) collective-permute-start(bf16[64,1280]{1,0:T(8,128)(2,1)S(1)} %collective-permute-done.2.refs_0_), channel_id=1, source_target_pairs={{0,3},{1,62},{2,1},{3,4},{4,7},{5,2},{6,5},{7,8},{8,11},{9,6},{10,... | collective-permute-start | bytes 491528 | tf_op jit(solution)/shard_map/ppermute | solution.py:190
  46.9 3.7 %collective-permute-start.4 = (bf16[64,1280]{1,0:T(8,128)(2,1)S(1)}, bf16[64,1280]{1,0:T(8,128)(2,1)S(1)}, u32[]{:S(2)}, u32[]{:S(2)}) collective-permute-start(bf16[64,1280]{1,0:T(8,128)(2,1)S(1)} %collective-permute-done.3.refs_2_), channel_id=1, source_target_pairs={{0,3},{1,62},{2,1},{3,4},{4,7},{5,2},{6,5},{7,8},{8,11},{9,6},{10,... | collective-permute-start | bytes 491528 | tf_op jit(solution)/shard_map/ppermute | solution.py:190
  52.9 3.7 %collective-permute-start.5 = (bf16[64,1280]{1,0:T(8,128)(2,1)S(1)}, bf16[64,1280]{1,0:T(8,128)(2,1)S(1)}, u32[]{:S(2)}, u32[]{:S(2)}) collective-permute-start(bf16[64,1280]{1,0:T(8,128)(2,1)S(1)} %collective-permute-done.4.refs_4_), channel_id=1, source_target_pairs={{0,3},{1,62},{2,1},{3,4},{4,7},{5,2},{6,5},{7,8},{8,11},{9,6},{10,... | collective-permute-start | bytes 491528 | tf_op jit(solution)/shard_map/ppermute | solution.py:190
  58.8 3.7 %collective-permute-start.6 = (bf16[64,1280]{1,0:T(8,128)(2,1)S(1)}, bf16[64,1280]{1,0:T(8,128)(2,1)S(1)}, u32[]{:S(2)}, u32[]{:S(2)}) collective-permute-start(bf16[64,1280]{1,0:T(8,128)(2,1)S(1)} %collective-permute-done.5.refs_0_), channel_id=1, source_target_pairs={{0,3},{1,62},{2,1},{3,4},{4,7},{5,2},{6,5},{7,8},{8,11},{9,6},{10,... | collective-permute-start | bytes 491528 | tf_op jit(solution)/shard_map/ppermute | solution.py:190
  64.8 3.7 %collective-permute-start.7 = (bf16[64,1280]{1,0:T(8,128)(2,1)S(1)}, bf16[64,1280]{1,0:T(8,128)(2,1)S(1)}, u32[]{:S(2)}, u32[]{:S(2)}) collective-permute-start(bf16[64,1280]{1,0:T(8,128)(2,1)S(1)} %collective-permute-done.6.refs_2_), channel_id=1, source_target_pairs={{0,3},{1,62},{2,1},{3,4},{4,7},{5,2},{6,5},{7,8},{8,11},{9,6},{10,... | collective-permute-start | bytes 491528 | tf_op jit(solution)/shard_map/ppermute | solution.py:190
  70.7 3.7 %collective-permute-start.8 = (bf16[64,1280]{1,0:T(8,128)(2,1)S(1)}, bf16[64,1280]{1,0:T(8,128)(2,1)S(1)}, u32[]{:S(2)}, u32[]{:S(2)}) collective-permute-start(bf16[64,1280]{1,0:T(8,128)(2,1)S(1)} %collective-permute-done.7.refs_4_), channel_id=1, source_target_pairs={{0,3},{1,62},{2,1},{3,4},{4,7},{5,2},{6,5},{7,8},{8,11},{9,6},{10,... | collective-permute-start | bytes 491528 | tf_op jit(solution)/shard_map/ppermute | solution.py:190
  76.7 3.7 %collective-permute-start.9 = (bf16[64,1280]{1,0:T(8,128)(2,1)S(1)}, bf16[64,1280]{1,0:T(8,128)(2,1)S(1)}, u32[]{:S(2)}, u32[]{:S(2)}) collective-permute-start(bf16[64,1280]{1,0:T(8,128)(2,1)S(1)} %collective-permute-done.8.refs_0_), channel_id=1, source_target_pairs={{0,3},{1,62},{2,1},{3,4},{4,7},{5,2},{6,5},{7,8},{8,11},{9,6},{10,... | collective-permute-start | bytes 491528 | tf_op jit(solution)/shard_map/ppermute | solution.py:190
  80.4 2.0 %collective-permute-start.38 = (bf16[256,1280]{1,0:T(8,128)(2,1)S(1)}, bf16[256,1280]{1,0:T(8,128)(2,1)S(1)}, u32[]{:S(2)}, u32[]{:S(2)}) collective-permute-start(bf16[256,1280]{1,0:T(8,128)(2,1)S(1)} %shard_map.81.refs_2_), channel_id=1, source_target_pairs={{0,129},{1,64},{2,67},{3,130},{4,133},{5,68},{6,71},{7,134},{8,137... | collective-permute-start | bytes 1966088 | tf_op jit(solution)/shard_map/ppermute | solution.py:199
  82.6 3.7 %collective-permute-start.10 = (bf16[64,1280]{1,0:T(8,128)(2,1)S(1)}, bf16[64,1280]{1,0:T(8,128)(2,1)S(1)}, u32[]{:S(2)}, u32[]{:S(2)}) collective-permute-start(bf16[64,1280]{1,0:T(8,128)(2,1)S(1)} %collective-permute-done.9.refs_2_), channel_id=1, source_target_pairs={{0,3},{1,62},{2,1},{3,4},{4,7},{5,2},{6,5},{7,8},{8,11},{9,6},{10,... | collective-permute-start | bytes 491528 | tf_op jit(solution)/shard_map/ppermute | solution.py:190
  86.4 2.0 %collective-permute-start.37 = (bf16[384,1280]{1,0:T(8,128)(2,1)S(1)}, bf16[384,1280]{1,0:T(8,128)(2,1)S(1)}, u32[]{:S(2)}, u32[]{:S(2)}) collective-permute-start(bf16[384,1280]{1,0:T(8,128)(2,1)S(1)} %shard_map.80.refs_2_), channel_id=1, source_target_pairs={{0,129},{1,64},{2,67},{3,130},{4,133},{5,68},{6,71},{7,134},{8,137... | collective-permute-start | bytes 2949128 | tf_op jit(solution)/shard_map/ppermute | solution.py:199
  89.2 3.0 %collective-permute-start.11 = (bf16[64,1280]{1,0:T(8,128)(2,1)S(1)}, bf16[64,1280]{1,0:T(8,128)(2,1)S(1)}, u32[]{:S(2)}, u32[]{:S(2)}) collective-permute-start(bf16[64,1280]{1,0:T(8,128)(2,1)S(1)} %collective-permute-done.10.refs_0_), channel_id=1, source_target_pairs={{0,3},{1,62},{2,1},{3,4},{4,7},{5,2},{6,5},{7,8},{8,11},{9,6},{10,... | collective-permute-start | bytes 491528 | tf_op jit(solution)/shard_map/ppermute | solution.py:190
  95.2 3.0 %collective-permute-start.12 = (bf16[64,1280]{1,0:T(8,128)(2,1)S(1)}, bf16[64,1280]{1,0:T(8,128)(2,1)S(1)}, u32[]{:S(2)}, u32[]{:S(2)}) collective-permute-start(bf16[64,1280]{1,0:T(8,128)(2,1)S(1)} %collective-permute-done.11.refs_2_), channel_id=1, source_target_pairs={{0,3},{1,62},{2,1},{3,4},{4,7},{5,2},{6,5},{7,8},{8,11},{9,6},{10,... | collective-permute-start | bytes 491528 | tf_op jit(solution)/shard_map/ppermute | solution.py:190
  98.2 2.1 %collective-permute-start.25 = (bf16[64,1280]{1,0:T(8,128)(2,1)S(1)}, bf16[64,1280]{1,0:T(8,128)(2,1)S(1)}, u32[]{:S(2)}, u32[]{:S(2)}) collective-permute-start(bf16[64,1280]{1,0:T(8,128)(2,1)S(1)} %collective-permute-done.24.refs_3_), channel_id=1, source_target_pairs={{0,3},{1,62},{2,1},{3,4},{4,7},{5,2},{6,5},{7,8},{8,11},{9,6},{10,... | collective-permute-start | bytes 491528 | tf_op jit(solution)/shard_map/ppermute | solution.py:191
  100.5 3.7 %collective-permute-start.26 = (bf16[64,1280]{1,0:T(8,128)(2,1)S(1)}, bf16[64,1280]{1,0:T(8,128)(2,1)S(1)}, u32[]{:S(2)}, u32[]{:S(2)}) collective-permute-start(bf16[64,1280]{1,0:T(8,128)(2,1)S(1)} %collective-permute-done.12.refs_0_), channel_id=1, source_target_pairs={{0,3},{1,62},{2,1},{3,4},{4,7},{5,2},{6,5},{7,8},{8,11},{9,6},{10,... | collective-permute-start | bytes 491528 | tf_op jit(solution)/shard_map/ppermute | solution.py:190
  104.3 2.0 %collective-permute-start.36 = (bf16[384,1280]{1,0:T(8,128)(2,1)S(1)}, bf16[384,1280]{1,0:T(8,128)(2,1)}, u32[]{:S(2)}, u32[]{:S(2)}) collective-permute-start(bf16[384,1280]{1,0:T(8,128)(2,1)S(1)} %shard_map.79.refs_2_), channel_id=1, source_target_pairs={{0,129},{1,64},{2,67},{3,130},{4,133},{5,68},{6,71},{7,134},{8,137... | collective-permute-start | bytes 2949128 | tf_op jit(solution)/shard_map/ppermute | solution.py:199
  106.5 3.7 %collective-permute-start.29 = (bf16[64,1280]{1,0:T(8,128)(2,1)S(1)}, bf16[64,1280]{1,0:T(8,128)(2,1)S(1)}, u32[]{:S(2)}, u32[]{:S(2)}) collective-permute-start(bf16[64,1280]{1,0:T(8,128)(2,1)S(1)} %collective-permute-done.26.refs_2_), channel_id=1, source_target_pairs={{0,3},{1,62},{2,1},{3,4},{4,7},{5,2},{6,5},{7,8},{8,11},{9,6},{10,... | collective-permute-start | bytes 491528 | tf_op jit(solution)/shard_map/ppermute | solution.py:190
  113.2 2.9 %collective-permute-start.31 = (bf16[64,1280]{1,0:T(8,128)(2,1)S(1)}, bf16[64,1280]{1,0:T(8,128)(2,1)S(1)}, u32[]{:S(2)}, u32[]{:S(2)}) collective-permute-start(bf16[64,1280]{1,0:T(8,128)(2,1)S(1)} %collective-permute-done.29.refs_0_), channel_id=1, source_target_pairs={{0,3},{1,62},{2,1},{3,4},{4,7},{5,2},{6,5},{7,8},{8,11},{9,6},{10,... | collective-permute-start | bytes 491528 | tf_op jit(solution)/shard_map/ppermute | solution.py:190
  128.3 3.3 %shard_map.87.refs_4_ = f32[384,1280]{1,0:T(8,128)S(1)} custom-call(s32[3]{0:T(128)S(1)} %pad_add_fusion.refs_0_, bf16[384,8192]{1,0:T(8,128)(2,1)} %collective-permute-done.39.refs_1_, bf16[256,1280]{1,0:T(8,128)(2,1)S(1)} %shard_map.81.refs_2_, bf16[256,1280]{1,0:T(8,128)(2,1)S(1)} %copy-done.3, bf16[128,1280]{1,0:T(8,128)(2,1)S(1)} %copy-done.5), custom_call_target="tpu_custom_call" | custom-call | flops 629145600 | bytes 6062080 | tf_op jit(solution)/shard_map/pallas_call | solution.py:106
  131.6 3.6 %shard_map.88.refs_4_ = f32[384,1280]{1,0:T(8,128)S(1)} custom-call(s32[3]{0:T(128)S(1)} %pad_add_fusion.refs_0_, bf16[384,8192]{1,0:T(8,128)(2,1)} %collective-permute-done.39.refs_1_, bf16[384,1280]{1,0:T(8,128)(2,1)S(1)} %shard_map.80.refs_2_, bf16[384,1280]{1,0:T(8,128)(2,1)S(1)} %copy-done.1, ...), custom_call_target="tpu_custom_call", output_to_operand_aliasing={{}: (4, {})} | custom-call | flops 754974720 | bytes 6488064 | tf_op jit(solution)/shard_map/pallas_call | solution.py:106
  135.2 4.5 %shard_map.89.refs_6_ = f32[384,1280]{1,0:T(8,128)S(1)} custom-call(s32[3]{0:T(128)S(1)} %pad_add_fusion.refs_0_, bf16[384,8192]{1,0:T(8,128)(2,1)} %collective-permute-done.39.refs_1_, bf16[384,1280]{1,0:T(8,128)(2,1)S(1)} %shard_map.79.refs_2_, bf16[384,1280]{1,0:T(8,128)(2,1)} %collective-permute-done.36.refs_3_, ...), custom_call_target="tpu_custom_call", output_to_operand_aliasing={{}: (4, {})} | custom-call | flops 754974720 | bytes 6488064 | tf_op jit(solution)/shard_map/pallas_call | solution.py:106
  139.8 4.8 %shard_map.90.refs_6_ = f32[384,1280]{1,0:T(8,128)S(1)} custom-call(s32[3]{0:T(128)S(1)} %pad_add_fusion.refs_0_, bf16[384,8192]{1,0:T(8,128)(2,1)} %collective-permute-done.39.refs_1_, bf16[256,1280]{1,0:T(8,128)(2,1)S(1)} %shard_map.77.refs_2_, bf16[256,1280]{1,0:T(8,128)(2,1)} %collective-permute-done.34.refs_3_, ...), custom_call_target="tpu_custom_call", output_to_operand_aliasing={{}: (6, {})} | custom-call | flops 1006632960 | bytes 7340032 | tf_op jit(solution)/shard_map/pallas_call | solution.py:106
  144.6 3.1 %collective-permute-done.33.refs_5_ = bf16[128,1280]{1,0:T(8,128)(2,1)S(1)} collective-permute-done((bf16[128,1280]{1,0:T(8,128)(2,1)S(1)}, bf16[128,1280]{1,0:T(8,128)(2,1)S(1)}, u32[]{:S(2)}, u32[]{:S(2)}) %collective-permute-start.33) | collective-permute-done | bytes 327712 | tf_op jit(solution)/shard_map/ppermute | solution.py:199
  147.7 4.5 %shard_map.91 = f32[384,1280]{1,0:T(8,128)S(1)} custom-call(s32[3]{0:T(128)S(1)} %pad_add_fusion.refs_0_, bf16[384,8192]{1,0:T(8,128)(2,1)} %collective-permute-done.39.refs_1_, bf16[256,1280]{1,0:T(8,128)(2,1)} %shard_map.74.refs_2_, bf16[256,1280]{1,0:T(8,128)(2,1)} %collective-permute-done.28.refs_3_, ...), custom_call_target="tpu_custom_call", output_to_operand_aliasing={{}: (6, {})} | custom-call | flops 880803840 | bytes 6914048 | tf_op jit(solution)/shard_map/pallas_call | solution.py:106
  152.4 2.4 %shard_map.82.refs_4_ = f32[384,1280]{1,0:T(8,128)S(1)} custom-call(s32[3]{0:T(128)S(1)} %pad_add_fusion.refs_0_, bf16[384,8192]{1,0:T(8,128)(2,1)S(1)} %bitcast.4, bf16[256,1280]{1,0:T(8,128)(2,1)S(1)} %shard_map.81.refs_2_, bf16[256,1280]{1,0:T(8,128)(2,1)S(1)} %copy-done.3, bf16[128,1280]{1,0:T(8,128)(2,1)S(1)} %copy-done.5), custom_call_target="tpu_custom_call" | custom-call | flops 629145600 | bytes 6062080 | tf_op jit(solution)/shard_map/pallas_call | solution.py:106
  154.8 2.6 %shard_map.83.refs_4_ = f32[384,1280]{1,0:T(8,128)S(1)} custom-call(s32[3]{0:T(128)S(1)} %pad_add_fusion.refs_0_, bf16[384,8192]{1,0:T(8,128)(2,1)S(1)} %bitcast.4, bf16[384,1280]{1,0:T(8,128)(2,1)S(1)} %shard_map.80.refs_2_, bf16[384,1280]{1,0:T(8,128)(2,1)S(1)} %copy-done.1, f32[384,1280]{1,0:T(8,128)S(1)} %shard_map.82.refs_4_), custom_call_target="tpu_custom_call", output_to_operand_aliasing={{}: (4, {})} | custom-call | flops 754974720 | bytes 6488064 | tf_op jit(solution)/shard_map/pallas_call | solution.py:106
  157.4 3.2 %shard_map.84.refs_6_ = f32[384,1280]{1,0:T(8,128)S(1)} custom-call(s32[3]{0:T(128)S(1)} %pad_add_fusion.refs_0_, bf16[384,8192]{1,0:T(8,128)(2,1)S(1)} %bitcast.4, bf16[384,1280]{1,0:T(8,128)(2,1)S(1)} %shard_map.79.refs_2_, bf16[384,1280]{1,0:T(8,128)(2,1)} %collective-permute-done.36.refs_3_, ...), custom_call_target="tpu_custom_call", output_to_operand_aliasing={{}: (4, {})} | custom-call | flops 754974720 | bytes 6488064 | tf_op jit(solution)/shard_map/pallas_call | solution.py:106
  160.6 3.7 %shard_map.85.refs_6_ = f32[384,1280]{1,0:T(8,128)S(1)} custom-call(s32[3]{0:T(128)S(1)} %pad_add_fusion.refs_0_, bf16[384,8192]{1,0:T(8,128)(2,1)S(1)} %bitcast.4, bf16[256,1280]{1,0:T(8,128)(2,1)S(1)} %shard_map.77.refs_2_, bf16[256,1280]{1,0:T(8,128)(2,1)} %collective-permute-done.34.refs_3_, ...), custom_call_target="tpu_custom_call", output_to_operand_aliasing={{}: (6, {})} | custom-call | flops 1006632960 | bytes 7340032 | tf_op jit(solution)/shard_map/pallas_call | solution.py:106
  164.4 3.5 %shard_map.86.acc_ref = f32[384,1280]{1,0:T(8,128)S(1)} custom-call(s32[3]{0:T(128)S(1)} %pad_add_fusion.refs_0_, bf16[384,8192]{1,0:T(8,128)(2,1)S(1)} %bitcast.4, bf16[256,1280]{1,0:T(8,128)(2,1)} %shard_map.74.refs_2_, bf16[256,1280]{1,0:T(8,128)(2,1)} %collective-permute-done.28.refs_3_, ...), custom_call_target="tpu_custom_call", output_to_operand_aliasing={{}: (6, {})} | custom-call | flops 880803840 | bytes 6914048 | tf_op jit(solution)/shard_map/pallas_call | solution.py:106
  (112 shorter events, 44.8 us)
Async XLA Ops:
  0.0 126.0 %collective-permute-start.39 = (bf16[384,8192]{1,0:T(8,128)(2,1)}, bf16[384,8192]{1,0:T(8,128)(2,1)}, u32[]{:S(2)}, u32[]{:S(2)}) collective-permute-start(bf16[384,8192]{1,0:T(8,128)(2,1)} %refs_1_.9), channel_id=1, source_target_pairs={{0,1},{1,0},{2,3},{3,2},{4,5},{5,4},{6,7},{7,6},{8,9},{9,8},{10,11... | collective-permute-start | bytes 18874376 | tf_op jit(solution)/shard_map/ppermute | solution.py:187
  26.8 6.0 %collective-permute-start.13 = (bf16[64,1280]{1,0:T(8,128)(2,1)S(1)}, bf16[64,1280]{1,0:T(8,128)(2,1)S(1)}, u32[]{:S(2)}, u32[]{:S(2)}) collective-permute-start(bf16[64,1280]{1,0:T(8,128)(2,1)S(1)} %get-tuple-element.9), channel_id=1, source_target_pairs={{0,3},{1,62},{2,1},{3,4},{4,7},{5,2},{6,5},{7,8},{8,11},{9,6},{10,... | collective-permute-start | bytes 491528 | tf_op jit(solution)/shard_map/ppermute | solution.py:191
  29.0 6.0 %collective-permute-start.1 = (bf16[64,1280]{1,0:T(8,128)(2,1)S(1)}, bf16[64,1280]{1,0:T(8,128)(2,1)S(1)}, u32[]{:S(2)}, u32[]{:S(2)}) collective-permute-start(bf16[64,1280]{1,0:T(8,128)(2,1)S(1)} %collective-permute-done.refs_0_), channel_id=1, source_target_pairs={{0,3},{1,62},{2,1},{3,4},{4,7},{5,2},{6,5},{7,8},{8,11},{9,6},{10,... | collective-permute-start | bytes 491528 | tf_op jit(solution)/shard_map/ppermute | solution.py:190
  32.7 6.0 %collective-permute-start.14 = (bf16[64,1280]{1,0:T(8,128)(2,1)S(1)}, bf16[64,1280]{1,0:T(8,128)(2,1)S(1)}, u32[]{:S(2)}, u32[]{:S(2)}) collective-permute-start(bf16[64,1280]{1,0:T(8,128)(2,1)S(1)} %collective-permute-done.13.refs_1_), channel_id=1, source_target_pairs={{0,3},{1,62},{2,1},{3,4},{4,7},{5,2},{6,5},{7,8},{8,11},{9,6},{10,... | collective-permute-start | bytes 491528 | tf_op jit(solution)/shard_map/ppermute | solution.py:191
  35.0 6.0 %collective-permute-start.2 = (bf16[64,1280]{1,0:T(8,128)(2,1)S(1)}, bf16[64,1280]{1,0:T(8,128)(2,1)S(1)}, u32[]{:S(2)}, u32[]{:S(2)}) collective-permute-start(bf16[64,1280]{1,0:T(8,128)(2,1)S(1)} %collective-permute-done.1.refs_2_), channel_id=1, source_target_pairs={{0,3},{1,62},{2,1},{3,4},{4,7},{5,2},{6,5},{7,8},{8,11},{9,6},{10,... | collective-permute-start | bytes 491528 | tf_op jit(solution)/shard_map/ppermute | solution.py:190
  38.7 6.0 %collective-permute-start.15 = (bf16[64,1280]{1,0:T(8,128)(2,1)S(1)}, bf16[64,1280]{1,0:T(8,128)(2,1)S(1)}, u32[]{:S(2)}, u32[]{:S(2)}) collective-permute-start(bf16[64,1280]{1,0:T(8,128)(2,1)S(1)} %collective-permute-done.14.refs_3_), channel_id=1, source_target_pairs={{0,3},{1,62},{2,1},{3,4},{4,7},{5,2},{6,5},{7,8},{8,11},{9,6},{10,... | collective-permute-start | bytes 491528 | tf_op jit(solution)/shard_map/ppermute | solution.py:191
  40.9 6.0 %collective-permute-start.3 = (bf16[64,1280]{1,0:T(8,128)(2,1)S(1)}, bf16[64,1280]{1,0:T(8,128)(2,1)S(1)}, u32[]{:S(2)}, u32[]{:S(2)}) collective-permute-start(bf16[64,1280]{1,0:T(8,128)(2,1)S(1)} %collective-permute-done.2.refs_0_), channel_id=1, source_target_pairs={{0,3},{1,62},{2,1},{3,4},{4,7},{5,2},{6,5},{7,8},{8,11},{9,6},{10,... | collective-permute-start | bytes 491528 | tf_op jit(solution)/shard_map/ppermute | solution.py:190
  46.9 6.0 %collective-permute-start.4 = (bf16[64,1280]{1,0:T(8,128)(2,1)S(1)}, bf16[64,1280]{1,0:T(8,128)(2,1)S(1)}, u32[]{:S(2)}, u32[]{:S(2)}) collective-permute-start(bf16[64,1280]{1,0:T(8,128)(2,1)S(1)} %collective-permute-done.3.refs_2_), channel_id=1, source_target_pairs={{0,3},{1,62},{2,1},{3,4},{4,7},{5,2},{6,5},{7,8},{8,11},{9,6},{10,... | collective-permute-start | bytes 491528 | tf_op jit(solution)/shard_map/ppermute | solution.py:190
  50.6 6.0 %collective-permute-start.17 = (bf16[64,1280]{1,0:T(8,128)(2,1)S(1)}, bf16[64,1280]{1,0:T(8,128)(2,1)S(1)}, u32[]{:S(2)}, u32[]{:S(2)}) collective-permute-start(bf16[64,1280]{1,0:T(8,128)(2,1)S(1)} %collective-permute-done.16.refs_3_), channel_id=1, source_target_pairs={{0,3},{1,62},{2,1},{3,4},{4,7},{5,2},{6,5},{7,8},{8,11},{9,6},{10,... | collective-permute-start | bytes 491528 | tf_op jit(solution)/shard_map/ppermute | solution.py:191
  52.9 6.0 %collective-permute-start.5 = (bf16[64,1280]{1,0:T(8,128)(2,1)S(1)}, bf16[64,1280]{1,0:T(8,128)(2,1)S(1)}, u32[]{:S(2)}, u32[]{:S(2)}) collective-permute-start(bf16[64,1280]{1,0:T(8,128)(2,1)S(1)} %collective-permute-done.4.refs_4_), channel_id=1, source_target_pairs={{0,3},{1,62},{2,1},{3,4},{4,7},{5,2},{6,5},{7,8},{8,11},{9,6},{10,... | collective-permute-start | bytes 491528 | tf_op jit(solution)/shard_map/ppermute | solution.py:190
  56.6 6.0 %collective-permute-start.18 = (bf16[64,1280]{1,0:T(8,128)(2,1)S(1)}, bf16[64,1280]{1,0:T(8,128)(2,1)S(1)}, u32[]{:S(2)}, u32[]{:S(2)}) collective-permute-start(bf16[64,1280]{1,0:T(8,128)(2,1)S(1)} %collective-permute-done.17.refs_5_), channel_id=1, source_target_pairs={{0,3},{1,62},{2,1},{3,4},{4,7},{5,2},{6,5},{7,8},{8,11},{9,6},{10,... | collective-permute-start | bytes 491528 | tf_op jit(solution)/shard_map/ppermute | solution.py:191
  58.8 6.0 %collective-permute-start.6 = (bf16[64,1280]{1,0:T(8,128)(2,1)S(1)}, bf16[64,1280]{1,0:T(8,128)(2,1)S(1)}, u32[]{:S(2)}, u32[]{:S(2)}) collective-permute-start(bf16[64,1280]{1,0:T(8,128)(2,1)S(1)} %collective-permute-done.5.refs_0_), channel_id=1, source_target_pairs={{0,3},{1,62},{2,1},{3,4},{4,7},{5,2},{6,5},{7,8},{8,11},{9,6},{10,... | collective-permute-start | bytes 491528 | tf_op jit(solution)/shard_map/ppermute | solution.py:190
  62.5 6.0 %collective-permute-start.19 = (bf16[64,1280]{1,0:T(8,128)(2,1)S(1)}, bf16[64,1280]{1,0:T(8,128)(2,1)S(1)}, u32[]{:S(2)}, u32[]{:S(2)}) collective-permute-start(bf16[64,1280]{1,0:T(8,128)(2,1)S(1)} %collective-permute-done.18.refs_1_), channel_id=1, source_target_pairs={{0,3},{1,62},{2,1},{3,4},{4,7},{5,2},{6,5},{7,8},{8,11},{9,6},{10,... | collective-permute-start | bytes 491528 | tf_op jit(solution)/shard_map/ppermute | solution.py:191
  64.8 6.0 %collective-permute-start.7 = (bf16[64,1280]{1,0:T(8,128)(2,1)S(1)}, bf16[64,1280]{1,0:T(8,128)(2,1)S(1)}, u32[]{:S(2)}, u32[]{:S(2)}) collective-permute-start(bf16[64,1280]{1,0:T(8,128)(2,1)S(1)} %collective-permute-done.6.refs_2_), channel_id=1, source_target_pairs={{0,3},{1,62},{2,1},{3,4},{4,7},{5,2},{6,5},{7,8},{8,11},{9,6},{10,... | collective-permute-start | bytes 491528 | tf_op jit(solution)/shard_map/ppermute | solution.py:190
  68.5 6.0 %collective-permute-start.20 = (bf16[64,1280]{1,0:T(8,128)(2,1)S(1)}, bf16[64,1280]{1,0:T(8,128)(2,1)S(1)}, u32[]{:S(2)}, u32[]{:S(2)}) collective-permute-start(bf16[64,1280]{1,0:T(8,128)(2,1)S(1)} %collective-permute-done.19.refs_3_), channel_id=1, source_target_pairs={{0,3},{1,62},{2,1},{3,4},{4,7},{5,2},{6,5},{7,8},{8,11},{9,6},{10,... | collective-permute-start | bytes 491528 | tf_op jit(solution)/shard_map/ppermute | solution.py:191
  70.7 6.0 %collective-permute-start.8 = (bf16[64,1280]{1,0:T(8,128)(2,1)S(1)}, bf16[64,1280]{1,0:T(8,128)(2,1)S(1)}, u32[]{:S(2)}, u32[]{:S(2)}) collective-permute-start(bf16[64,1280]{1,0:T(8,128)(2,1)S(1)} %collective-permute-done.7.refs_4_), channel_id=1, source_target_pairs={{0,3},{1,62},{2,1},{3,4},{4,7},{5,2},{6,5},{7,8},{8,11},{9,6},{10,... | collective-permute-start | bytes 491528 | tf_op jit(solution)/shard_map/ppermute | solution.py:190
  74.4 8.0 %collective-permute-start.21 = (bf16[64,1280]{1,0:T(8,128)(2,1)S(1)}, bf16[64,1280]{1,0:T(8,128)(2,1)S(1)}, u32[]{:S(2)}, u32[]{:S(2)}) collective-permute-start(bf16[64,1280]{1,0:T(8,128)(2,1)S(1)} %collective-permute-done.20.refs_5_), channel_id=1, source_target_pairs={{0,3},{1,62},{2,1},{3,4},{4,7},{5,2},{6,5},{7,8},{8,11},{9,6},{10,... | collective-permute-start | bytes 491528 | tf_op jit(solution)/shard_map/ppermute | solution.py:191
  80.4 23.8 %collective-permute-start.38 = (bf16[256,1280]{1,0:T(8,128)(2,1)S(1)}, bf16[256,1280]{1,0:T(8,128)(2,1)S(1)}, u32[]{:S(2)}, u32[]{:S(2)}) collective-permute-start(bf16[256,1280]{1,0:T(8,128)(2,1)S(1)} %shard_map.81.refs_2_), channel_id=1, source_target_pairs={{0,129},{1,64},{2,67},{3,130},{4,133},{5,68},{6,71},{7,134},{8,137... | collective-permute-start | bytes 1966088 | tf_op jit(solution)/shard_map/ppermute | solution.py:199
  82.4 6.0 %collective-permute-start.22 = (bf16[64,1280]{1,0:T(8,128)(2,1)S(1)}, bf16[64,1280]{1,0:T(8,128)(2,1)S(1)}, u32[]{:S(2)}, u32[]{:S(2)}) collective-permute-start(bf16[64,1280]{1,0:T(8,128)(2,1)S(1)} %collective-permute-done.21.refs_1_), channel_id=1, source_target_pairs={{0,3},{1,62},{2,1},{3,4},{4,7},{5,2},{6,5},{7,8},{8,11},{9,6},{10,... | collective-permute-start | bytes 491528 | tf_op jit(solution)/shard_map/ppermute | solution.py:191
  82.6 6.6 %collective-permute-start.10 = (bf16[64,1280]{1,0:T(8,128)(2,1)S(1)}, bf16[64,1280]{1,0:T(8,128)(2,1)S(1)}, u32[]{:S(2)}, u32[]{:S(2)}) collective-permute-start(bf16[64,1280]{1,0:T(8,128)(2,1)S(1)} %collective-permute-done.9.refs_2_), channel_id=1, source_target_pairs={{0,3},{1,62},{2,1},{3,4},{4,7},{5,2},{6,5},{7,8},{8,11},{9,6},{10,... | collective-permute-start | bytes 491528 | tf_op jit(solution)/shard_map/ppermute | solution.py:190
  86.4 32.8 %collective-permute-start.37 = (bf16[384,1280]{1,0:T(8,128)(2,1)S(1)}, bf16[384,1280]{1,0:T(8,128)(2,1)S(1)}, u32[]{:S(2)}, u32[]{:S(2)}) collective-permute-start(bf16[384,1280]{1,0:T(8,128)(2,1)S(1)} %shard_map.80.refs_2_), channel_id=1, source_target_pairs={{0,129},{1,64},{2,67},{3,130},{4,133},{5,68},{6,71},{7,134},{8,137... | collective-permute-start | bytes 2949128 | tf_op jit(solution)/shard_map/ppermute | solution.py:199
  89.2 6.0 %collective-permute-start.11 = (bf16[64,1280]{1,0:T(8,128)(2,1)S(1)}, bf16[64,1280]{1,0:T(8,128)(2,1)S(1)}, u32[]{:S(2)}, u32[]{:S(2)}) collective-permute-start(bf16[64,1280]{1,0:T(8,128)(2,1)S(1)} %collective-permute-done.10.refs_0_), channel_id=1, source_target_pairs={{0,3},{1,62},{2,1},{3,4},{4,7},{5,2},{6,5},{7,8},{8,11},{9,6},{10,... | collective-permute-start | bytes 491528 | tf_op jit(solution)/shard_map/ppermute | solution.py:190
  98.2 8.1 %collective-permute-start.25 = (bf16[64,1280]{1,0:T(8,128)(2,1)S(1)}, bf16[64,1280]{1,0:T(8,128)(2,1)S(1)}, u32[]{:S(2)}, u32[]{:S(2)}) collective-permute-start(bf16[64,1280]{1,0:T(8,128)(2,1)S(1)} %collective-permute-done.24.refs_3_), channel_id=1, source_target_pairs={{0,3},{1,62},{2,1},{3,4},{4,7},{5,2},{6,5},{7,8},{8,11},{9,6},{10,... | collective-permute-start | bytes 491528 | tf_op jit(solution)/shard_map/ppermute | solution.py:191
  104.3 30.9 %collective-permute-start.36 = (bf16[384,1280]{1,0:T(8,128)(2,1)S(1)}, bf16[384,1280]{1,0:T(8,128)(2,1)}, u32[]{:S(2)}, u32[]{:S(2)}) collective-permute-start(bf16[384,1280]{1,0:T(8,128)(2,1)S(1)} %shard_map.79.refs_2_), channel_id=1, source_target_pairs={{0,129},{1,64},{2,67},{3,130},{4,133},{5,68},{6,71},{7,134},{8,137... | collective-permute-start | bytes 2949128 | tf_op jit(solution)/shard_map/ppermute | solution.py:199
  106.5 6.8 %collective-permute-start.29 = (bf16[64,1280]{1,0:T(8,128)(2,1)S(1)}, bf16[64,1280]{1,0:T(8,128)(2,1)S(1)}, u32[]{:S(2)}, u32[]{:S(2)}) collective-permute-start(bf16[64,1280]{1,0:T(8,128)(2,1)S(1)} %collective-permute-done.26.refs_2_), channel_id=1, source_target_pairs={{0,3},{1,62},{2,1},{3,4},{4,7},{5,2},{6,5},{7,8},{8,11},{9,6},{10,... | collective-permute-start | bytes 491528 | tf_op jit(solution)/shard_map/ppermute | solution.py:190
  113.2 8.5 %collective-permute-start.31 = (bf16[64,1280]{1,0:T(8,128)(2,1)S(1)}, bf16[64,1280]{1,0:T(8,128)(2,1)S(1)}, u32[]{:S(2)}, u32[]{:S(2)}) collective-permute-start(bf16[64,1280]{1,0:T(8,128)(2,1)S(1)} %collective-permute-done.29.refs_0_), channel_id=1, source_target_pairs={{0,3},{1,62},{2,1},{3,4},{4,7},{5,2},{6,5},{7,8},{8,11},{9,6},{10,... | collective-permute-start | bytes 491528 | tf_op jit(solution)/shard_map/ppermute | solution.py:190
  116.2 6.6 %collective-permute-start.32 = (bf16[64,1280]{1,0:T(8,128)(2,1)S(1)}, bf16[64,1280]{1,0:T(8,128)(2,1)S(1)}, u32[]{:S(2)}, u32[]{:S(2)}) collective-permute-start(bf16[64,1280]{1,0:T(8,128)(2,1)S(1)} %collective-permute-done.30.refs_1_), channel_id=1, source_target_pairs={{0,3},{1,62},{2,1},{3,4},{4,7},{5,2},{6,5},{7,8},{8,11},{9,6},{10,... | collective-permute-start | bytes 491528 | tf_op jit(solution)/shard_map/ppermute | solution.py:191
  120.2 19.6 %collective-permute-start.34 = (bf16[256,1280]{1,0:T(8,128)(2,1)S(1)}, bf16[256,1280]{1,0:T(8,128)(2,1)}, u32[]{:S(2)}, u32[]{:S(2)}) collective-permute-start(bf16[256,1280]{1,0:T(8,128)(2,1)S(1)} %shard_map.77.refs_2_), channel_id=1, source_target_pairs={{0,129},{1,64},{2,67},{3,130},{4,133},{5,68},{6,71},{7,134},{8,137... | collective-permute-start | bytes 1966088 | tf_op jit(solution)/shard_map/ppermute | solution.py:199
  121.7 18.1 %collective-permute-start.35 = (bf16[256,1280]{1,0:T(8,128)(2,1)}, bf16[256,1280]{1,0:T(8,128)(2,1)}, u32[]{:S(2)}, u32[]{:S(2)}) collective-permute-start(bf16[256,1280]{1,0:T(8,128)(2,1)} %shard_map.78.refs_4_), channel_id=1, source_target_pairs={{0,129},{1,64},{2,67},{3,130},{4,133},{5,68},{6,71},{7,134},{8,137... | collective-permute-start | bytes 1966088 | tf_op jit(solution)/shard_map/ppermute | solution.py:199
  123.5 24.3 %collective-permute-start.28 = (bf16[256,1280]{1,0:T(8,128)(2,1)}, bf16[256,1280]{1,0:T(8,128)(2,1)}, u32[]{:S(2)}, u32[]{:S(2)}) collective-permute-start(bf16[256,1280]{1,0:T(8,128)(2,1)} %shard_map.74.refs_2_), channel_id=1, source_target_pairs={{0,129},{1,64},{2,67},{3,130},{4,133},{5,68},{6,71},{7,134},{8,137... | collective-permute-start | bytes 1966088 | tf_op jit(solution)/shard_map/ppermute | solution.py:199
  126.0 21.8 %collective-permute-start.33 = (bf16[128,1280]{1,0:T(8,128)(2,1)S(1)}, bf16[128,1280]{1,0:T(8,128)(2,1)S(1)}, u32[]{:S(2)}, u32[]{:S(2)}) collective-permute-start(bf16[128,1280]{1,0:T(8,128)(2,1)S(1)} %shard_map.76), channel_id=1, source_target_pairs={{0,129},{1,64},{2,67},{3,130},{4,133},{5,68},{6,71},{7,134},{8,137... | collective-permute-start | bytes 983048 | tf_op jit(solution)/shard_map/ppermute | solution.py:199
  152.2 15.7 %collective-permute-start.40 = (f32[384,1280]{1,0:T(8,128)S(1)}, f32[384,1280]{1,0:T(8,128)S(1)}, u32[]{:S(2)}, u32[]{:S(2)}) collective-permute-start(f32[384,1280]{1,0:T(8,128)S(1)} %shard_map.91), channel_id=1, source_target_pairs={{0,1},{1,0},{2,3},{3,2},{4,5},{5,4},{6,7},{7,6},{8,9},{9,8},{10,11... | collective-permute-start | bytes 5898248 | tf_op jit(solution)/shard_map/ppermute | solution.py:210
  (29 other events, 134.3 us)
where the time goes:
time: 170 us
  starting transfers between devices  108 us (64%)
  Pallas kernels  40.2 us (24%)
  waiting for transfers between devices  14.2 us (8%)
  local copies, waits for them, and re-layouts  7.03 us (4%)
    ppermute x16, starting transfers between devices, local(): a = lax.ppermute(a, both, along)  56.9 us
    pallas_call x10, Pallas kernels, accumulate(): pl.pallas_call(lambda *refs: accumulate_kernel(sources, len(parts), first...  36.2 us
    ppermute x16, starting transfers between devices, local(): b = lax.ppermute(b, both, along)  20.8 us
    ppermute x1, starting transfers between devices, local(): theirs = lax.ppermute(tokens, 'dp', mate)  20.4 us
    ppermute x7, starting transfers between devices, local(): got = lax.ppermute(near, both, across)  9.69 us
    ppermute x16, waiting for transfers between devices, local(): a = lax.ppermute(a, both, along)  8.49 us
    unnamed x40, local copies, waits for them, and re-layouts  7.03 us
  transfers between devices with their start and end apart: 41, of which 19 were waited for; matrix products, arithmetic and copies ran while one was open for 0% of the time, Pallas kernels for 20%

commit v1 on v0

--- a/solution.py
+++ b/solution.py
@@ -62,10 +62,7 @@
     )(*pieces)
 
 
-def accumulate_kernel(sources, part_count, first, chips, where_ref, tokens_ref, *refs):
-    parts = refs[:part_count]
-    acc_in = None if first else refs[part_count]
-    out_ref, tok, sem = refs[part_count + (0 if first else 1) :]
+def fetch(sources, chips, where_ref, tokens_ref, tok, sem):
     chip, sign, core = where_ref[0], where_ref[1], where_ref[2]
     copies = []
     for k, (distance, mine) in enumerate(sources):
@@ -84,6 +81,28 @@
     for copy in copies:
         copy.wait()
 
+
+def gather(tokens, where, chips, sources):
+    n = len(sources)
+    return pl.pallas_call(
+        lambda *refs: fetch(sources, chips, *refs),
+        out_shape=jax.ShapeDtypeStruct((tokens.shape[0], n * BLOCK), tokens.dtype),
+        in_specs=[SMEM, ANY],
+        out_specs=VMEM,
+        scratch_shapes=[pltpu.SemaphoreType.DMA((n,))],
+        compiler_params=pltpu.CompilerParams(vmem_limit_bytes=LIMIT),
+        cost_estimate=pl.CostEstimate(flops=2**20, bytes_accessed=4 * tokens.shape[0] * n * BLOCK, transcendentals=0),
+    )(where, tokens)
+
+
+def accumulate_kernel(sources, part_count, first, ready, chips, where_ref, tokens_ref, *refs):
+    parts = refs[:part_count]
+    acc_in = None if first else refs[part_count]
+    out_ref, *scratch = refs[part_count + (0 if first else 1) :]
+    tok = tokens_ref if ready else scratch[0]
+    if not ready:
+        fetch(sources, chips, where_ref, tokens_ref, *scratch)
+
     def column_tile(k, carry):
         at = pl.ds(pl.multiple_of(k * TILE, TILE), TILE)
         total = None if first else acc_in[:, at]
@@ -99,17 +118,19 @@
     lax.fori_loop(0, out_ref.shape[1] // TILE, column_tile, 0)
 
 
-def accumulate(acc, tokens, where, chips, sources, parts, dtype=jnp.float32):
+def accumulate(acc, tokens, where, chips, sources, parts, ready=False):
     rows, width = tokens.shape[0], parts[0].shape[1]
     first = acc is None
     n = len(sources)
     return pl.pallas_call(
-        lambda *refs: accumulate_kernel(sources, len(parts), first, chips, *refs),
-        out_shape=jax.ShapeDtypeStruct((rows, width), dtype),
-        in_specs=[SMEM, ANY] + [VMEM] * (len(parts) + (0 if first else 1)),
-        out_specs=VMEM,
-        input_output_aliases={} if first or dtype != acc.dtype else {2 + len(parts): 0},
-        scratch_shapes=[pltpu.VMEM((rows, n * BLOCK), jnp.bfloat16), pltpu.SemaphoreType.DMA((n,))],
+        lambda *refs: accumulate_kernel(sources, len(parts), first, ready, chips, *refs),
+        out_shape=jax.ShapeDtypeStruct((rows, width), jnp.float32),
+        in_specs=[SMEM, VMEM if ready else ANY] + [VMEM] * (len(parts) + (0 if first else 1)),
+        out_specs=VMEM,
+        input_output_aliases={} if first else {2 + len(parts): 0},
+        scratch_shapes=[]
+        if ready
+        else [pltpu.VMEM((rows, n * BLOCK), jnp.bfloat16), pltpu.SemaphoreType.DMA((n,))],
         compiler_params=pltpu.CompilerParams(vmem_limit_bytes=LIMIT),
         cost_estimate=pl.CostEstimate(
             flops=2 * rows * n * BLOCK * width,
@@ -205,7 +226,10 @@
                 sources += mine + [(s, False) for s in steps]
             if k == 0:
                 parts, sources = parts + [own], sources + [(0, True)]
-            acc_theirs = accumulate(acc_theirs, theirs, where, chips, sources, parts)
+            final = k == len(GROUPS) - 1
+            if final:
+                theirs = gather(theirs, where, chips, sources)
+            acc_theirs = accumulate(acc_theirs, theirs, where, chips, sources, parts, final)
             acc = accumulate(acc, tokens, where, chips, sources, parts)
         rest = lax.ppermute(acc_theirs, "dp", mate)
         return finish(acc, rest, up_stack, adapter_scale, lengths, adapter_ids)

time: 170 us -> 169 us (level)
  waiting for transfers between devices: 14.2 us -> 12.4 us
    ppermute x7, waiting for transfers between devices: 3.12 us -> 1.28 us  [local(): got = lax.ppermute(near, both, across)]
    pallas_call x0 -> x1, Pallas kernels: none -> 1.82 us  [gather(): pl.pallas_call(lambda *refs: fetch(sources, chips, *refs), out_shape=jax....]
  transfers between devices with their start and end apart: 41 -> 41, of which waited for: 19 -> 19; matrix products, arithmetic and copies ran while one was open for 0% -> 0% of each run, Pallas kernels for 20% -> 21%
where the time goes in v1:
time: 169 us
  starting transfers between devices  108 us (64%)
  Pallas kernels  40.8 us (24%)
  waiting for transfers between devices  12.4 us (7%)
  local copies, waits for them, and re-layouts  7.03 us (4%)
    ppermute x16, starting transfers between devices, local(): a = lax.ppermute(a, both, along)  56.9 us
    pallas_call x10, Pallas kernels, accumulate(): pl.pallas_call(lambda *refs: accumulate_kernel(sources, len(parts), first...  34.9 us
    ppermute x16, starting transfers between devices, local(): b = lax.ppermute(b, both, along)  20.8 us
    ppermute x1, starting transfers between devices, local(): theirs = lax.ppermute(tokens, 'dp', mate)  20.4 us
    ppermute x7, starting transfers between devices, local(): got = lax.ppermute(near, both, across)  9.69 us
    ppermute x16, waiting for transfers between devices, local(): a = lax.ppermute(a, both, along)  8.49 us
    unnamed x40, local copies, waits for them, and re-layouts  7.03 us
  transfers between devices with their start and end apart: 41, of which 19 were waited for; matrix products, arithmetic and copies ran while one was open for 0% of the time, Pallas kernels for 21%

profile of v1, /device:TPU:37, one launch (start us, length us, event | category | flops | bytes accessed | tf_op | source)
XLA Modules:
  0.0 168.6 jit_solution(8903966377307550645)
XLA Ops:
  0.0 20.4 %collective-permute-start.39 = (bf16[384,8192]{1,0:T(8,128)(2,1)}, bf16[384,8192]{1,0:T(8,128)(2,1)}, u32[]{:S(2)}, u32[]{:S(2)}) collective-permute-start(bf16[384,8192]{1,0:T(8,128)(2,1)} %refs_1_.9), channel_id=1, source_target_pairs={{0,1},{1,0},{2,3},{3,2},{4,5},{5,4},{6,7},{7,6},{8,9},{9,8},{10,11... | collective-permute-start | bytes 18874376 | tf_op jit(solution)/shard_map/ppermute | solution.py:208
  23.1 3.7 %collective-permute-start = (bf16[64,1280]{1,0:T(8,128)(2,1)S(1)}, bf16[64,1280]{1,0:T(8,128)(2,1)S(1)}, u32[]{:S(2)}, u32[]{:S(2)}) collective-permute-start(bf16[64,1280]{1,0:T(8,128)(2,1)S(1)} %get-tuple-element.8), channel_id=1, source_target_pairs={{0,3},{1,62},{2,1},{3,4},{4,7},{5,2},{6,5},{7,8},{8,11},{9,6},{10,... | collective-permute-start | bytes 491528 | tf_op jit(solution)/shard_map/ppermute | solution.py:211
  29.0 3.7 %collective-permute-start.1 = (bf16[64,1280]{1,0:T(8,128)(2,1)S(1)}, bf16[64,1280]{1,0:T(8,128)(2,1)S(1)}, u32[]{:S(2)}, u32[]{:S(2)}) collective-permute-start(bf16[64,1280]{1,0:T(8,128)(2,1)S(1)} %collective-permute-done.refs_0_), channel_id=1, source_target_pairs={{0,3},{1,62},{2,1},{3,4},{4,7},{5,2},{6,5},{7,8},{8,11},{9,6},{10,... | collective-permute-start | bytes 491528 | tf_op jit(solution)/shard_map/ppermute | solution.py:211
  35.0 3.7 %collective-permute-start.2 = (bf16[64,1280]{1,0:T(8,128)(2,1)S(1)}, bf16[64,1280]{1,0:T(8,128)(2,1)S(1)}, u32[]{:S(2)}, u32[]{:S(2)}) collective-permute-start(bf16[64,1280]{1,0:T(8,128)(2,1)S(1)} %collective-permute-done.1.refs_2_), channel_id=1, source_target_pairs={{0,3},{1,62},{2,1},{3,4},{4,7},{5,2},{6,5},{7,8},{8,11},{9,6},{10,... | collective-permute-start | bytes 491528 | tf_op jit(solution)/shard_map/ppermute | solution.py:211
  40.9 3.7 %collective-permute-start.3 = (bf16[64,1280]{1,0:T(8,128)(2,1)S(1)}, bf16[64,1280]{1,0:T(8,128)(2,1)S(1)}, u32[]{:S(2)}, u32[]{:S(2)}) collective-permute-start(bf16[64,1280]{1,0:T(8,128)(2,1)S(1)} %collective-permute-done.2.refs_0_), channel_id=1, source_target_pairs={{0,3},{1,62},{2,1},{3,4},{4,7},{5,2},{6,5},{7,8},{8,11},{9,6},{10,... | collective-permute-start | bytes 491528 | tf_op jit(solution)/shard_map/ppermute | solution.py:211
  46.9 3.7 %collective-permute-start.4 = (bf16[64,1280]{1,0:T(8,128)(2,1)S(1)}, bf16[64,1280]{1,0:T(8,128)(2,1)S(1)}, u32[]{:S(2)}, u32[]{:S(2)}) collective-permute-start(bf16[64,1280]{1,0:T(8,128)(2,1)S(1)} %collective-permute-done.3.refs_2_), channel_id=1, source_target_pairs={{0,3},{1,62},{2,1},{3,4},{4,7},{5,2},{6,5},{7,8},{8,11},{9,6},{10,... | collective-permute-start | bytes 491528 | tf_op jit(solution)/shard_map/ppermute | solution.py:211
  52.9 3.7 %collective-permute-start.5 = (bf16[64,1280]{1,0:T(8,128)(2,1)S(1)}, bf16[64,1280]{1,0:T(8,128)(2,1)S(1)}, u32[]{:S(2)}, u32[]{:S(2)}) collective-permute-start(bf16[64,1280]{1,0:T(8,128)(2,1)S(1)} %collective-permute-done.4.refs_4_), channel_id=1, source_target_pairs={{0,3},{1,62},{2,1},{3,4},{4,7},{5,2},{6,5},{7,8},{8,11},{9,6},{10,... | collective-permute-start | bytes 491528 | tf_op jit(solution)/shard_map/ppermute | solution.py:211
  58.8 3.7 %collective-permute-start.6 = (bf16[64,1280]{1,0:T(8,128)(2,1)S(1)}, bf16[64,1280]{1,0:T(8,128)(2,1)S(1)}, u32[]{:S(2)}, u32[]{:S(2)}) collective-permute-start(bf16[64,1280]{1,0:T(8,128)(2,1)S(1)} %collective-permute-done.5.refs_0_), channel_id=1, source_target_pairs={{0,3},{1,62},{2,1},{3,4},{4,7},{5,2},{6,5},{7,8},{8,11},{9,6},{10,... | collective-permute-start | bytes 491528 | tf_op jit(solution)/shard_map/ppermute | solution.py:211
  64.8 3.7 %collective-permute-start.7 = (bf16[64,1280]{1,0:T(8,128)(2,1)S(1)}, bf16[64,1280]{1,0:T(8,128)(2,1)S(1)}, u32[]{:S(2)}, u32[]{:S(2)}) collective-permute-start(bf16[64,1280]{1,0:T(8,128)(2,1)S(1)} %collective-permute-done.6.refs_2_), channel_id=1, source_target_pairs={{0,3},{1,62},{2,1},{3,4},{4,7},{5,2},{6,5},{7,8},{8,11},{9,6},{10,... | collective-permute-start | bytes 491528 | tf_op jit(solution)/shard_map/ppermute | solution.py:211
  70.7 3.7 %collective-permute-start.8 = (bf16[64,1280]{1,0:T(8,128)(2,1)S(1)}, bf16[64,1280]{1,0:T(8,128)(2,1)S(1)}, u32[]{:S(2)}, u32[]{:S(2)}) collective-permute-start(bf16[64,1280]{1,0:T(8,128)(2,1)S(1)} %collective-permute-done.7.refs_4_), channel_id=1, source_target_pairs={{0,3},{1,62},{2,1},{3,4},{4,7},{5,2},{6,5},{7,8},{8,11},{9,6},{10,... | collective-permute-start | bytes 491528 | tf_op jit(solution)/shard_map/ppermute | solution.py:211
  76.7 3.7 %collective-permute-start.9 = (bf16[64,1280]{1,0:T(8,128)(2,1)S(1)}, bf16[64,1280]{1,0:T(8,128)(2,1)S(1)}, u32[]{:S(2)}, u32[]{:S(2)}) collective-permute-start(bf16[64,1280]{1,0:T(8,128)(2,1)S(1)} %collective-permute-done.8.refs_0_), channel_id=1, source_target_pairs={{0,3},{1,62},{2,1},{3,4},{4,7},{5,2},{6,5},{7,8},{8,11},{9,6},{10,... | collective-permute-start | bytes 491528 | tf_op jit(solution)/shard_map/ppermute | solution.py:211
  80.4 2.0 %collective-permute-start.38 = (bf16[256,1280]{1,0:T(8,128)(2,1)S(1)}, bf16[256,1280]{1,0:T(8,128)(2,1)S(1)}, u32[]{:S(2)}, u32[]{:S(2)}) collective-permute-start(bf16[256,1280]{1,0:T(8,128)(2,1)S(1)} %shard_map.81.refs_2_), channel_id=1, source_target_pairs={{0,129},{1,64},{2,67},{3,130},{4,133},{5,68},{6,71},{7,134},{8,137... | collective-permute-start | bytes 1966088 | tf_op jit(solution)/shard_map/ppermute | solution.py:220
  82.6 3.7 %collective-permute-start.10 = (bf16[64,1280]{1,0:T(8,128)(2,1)S(1)}, bf16[64,1280]{1,0:T(8,128)(2,1)S(1)}, u32[]{:S(2)}, u32[]{:S(2)}) collective-permute-start(bf16[64,1280]{1,0:T(8,128)(2,1)S(1)} %collective-permute-done.9.refs_2_), channel_id=1, source_target_pairs={{0,3},{1,62},{2,1},{3,4},{4,7},{5,2},{6,5},{7,8},{8,11},{9,6},{10,... | collective-permute-start | bytes 491528 | tf_op jit(solution)/shard_map/ppermute | solution.py:211
  86.4 2.0 %collective-permute-start.37 = (bf16[384,1280]{1,0:T(8,128)(2,1)S(1)}, bf16[384,1280]{1,0:T(8,128)(2,1)S(1)}, u32[]{:S(2)}, u32[]{:S(2)}) collective-permute-start(bf16[384,1280]{1,0:T(8,128)(2,1)S(1)} %shard_map.80.refs_2_), channel_id=1, source_target_pairs={{0,129},{1,64},{2,67},{3,130},{4,133},{5,68},{6,71},{7,134},{8,137... | collective-permute-start | bytes 2949128 | tf_op jit(solution)/shard_map/ppermute | solution.py:220
  89.2 3.0 %collective-permute-start.11 = (bf16[64,1280]{1,0:T(8,128)(2,1)S(1)}, bf16[64,1280]{1,0:T(8,128)(2,1)S(1)}, u32[]{:S(2)}, u32[]{:S(2)}) collective-permute-start(bf16[64,1280]{1,0:T(8,128)(2,1)S(1)} %collective-permute-done.10.refs_0_), channel_id=1, source_target_pairs={{0,3},{1,62},{2,1},{3,4},{4,7},{5,2},{6,5},{7,8},{8,11},{9,6},{10,... | collective-permute-start | bytes 491528 | tf_op jit(solution)/shard_map/ppermute | solution.py:211
  95.2 3.0 %collective-permute-start.12 = (bf16[64,1280]{1,0:T(8,128)(2,1)S(1)}, bf16[64,1280]{1,0:T(8,128)(2,1)S(1)}, u32[]{:S(2)}, u32[]{:S(2)}) collective-permute-start(bf16[64,1280]{1,0:T(8,128)(2,1)S(1)} %collective-permute-done.11.refs_2_), channel_id=1, source_target_pairs={{0,3},{1,62},{2,1},{3,4},{4,7},{5,2},{6,5},{7,8},{8,11},{9,6},{10,... | collective-permute-start | bytes 491528 | tf_op jit(solution)/shard_map/ppermute | solution.py:211
  98.2 2.1 %collective-permute-start.25 = (bf16[64,1280]{1,0:T(8,128)(2,1)S(1)}, bf16[64,1280]{1,0:T(8,128)(2,1)S(1)}, u32[]{:S(2)}, u32[]{:S(2)}) collective-permute-start(bf16[64,1280]{1,0:T(8,128)(2,1)S(1)} %collective-permute-done.24.refs_3_), channel_id=1, source_target_pairs={{0,3},{1,62},{2,1},{3,4},{4,7},{5,2},{6,5},{7,8},{8,11},{9,6},{10,... | collective-permute-start | bytes 491528 | tf_op jit(solution)/shard_map/ppermute | solution.py:212
  100.5 3.7 %collective-permute-start.26 = (bf16[64,1280]{1,0:T(8,128)(2,1)S(1)}, bf16[64,1280]{1,0:T(8,128)(2,1)S(1)}, u32[]{:S(2)}, u32[]{:S(2)}) collective-permute-start(bf16[64,1280]{1,0:T(8,128)(2,1)S(1)} %collective-permute-done.12.refs_0_), channel_id=1, source_target_pairs={{0,3},{1,62},{2,1},{3,4},{4,7},{5,2},{6,5},{7,8},{8,11},{9,6},{10,... | collective-permute-start | bytes 491528 | tf_op jit(solution)/shard_map/ppermute | solution.py:211
  104.3 2.0 %collective-permute-start.36 = (bf16[384,1280]{1,0:T(8,128)(2,1)S(1)}, bf16[384,1280]{1,0:T(8,128)(2,1)}, u32[]{:S(2)}, u32[]{:S(2)}) collective-permute-start(bf16[384,1280]{1,0:T(8,128)(2,1)S(1)} %shard_map.79.refs_2_), channel_id=1, source_target_pairs={{0,129},{1,64},{2,67},{3,130},{4,133},{5,68},{6,71},{7,134},{8,137... | collective-permute-start | bytes 2949128 | tf_op jit(solution)/shard_map/ppermute | solution.py:220
  106.5 3.7 %collective-permute-start.29 = (bf16[64,1280]{1,0:T(8,128)(2,1)S(1)}, bf16[64,1280]{1,0:T(8,128)(2,1)S(1)}, u32[]{:S(2)}, u32[]{:S(2)}) collective-permute-start(bf16[64,1280]{1,0:T(8,128)(2,1)S(1)} %collective-permute-done.26.refs_2_), channel_id=1, source_target_pairs={{0,3},{1,62},{2,1},{3,4},{4,7},{5,2},{6,5},{7,8},{8,11},{9,6},{10,... | collective-permute-start | bytes 491528 | tf_op jit(solution)/shard_map/ppermute | solution.py:211
  113.2 2.9 %collective-permute-start.31 = (bf16[64,1280]{1,0:T(8,128)(2,1)S(1)}, bf16[64,1280]{1,0:T(8,128)(2,1)S(1)}, u32[]{:S(2)}, u32[]{:S(2)}) collective-permute-start(bf16[64,1280]{1,0:T(8,128)(2,1)S(1)} %collective-permute-done.29.refs_0_), channel_id=1, source_target_pairs={{0,3},{1,62},{2,1},{3,4},{4,7},{5,2},{6,5},{7,8},{8,11},{9,6},{10,... | collective-permute-start | bytes 491528 | tf_op jit(solution)/shard_map/ppermute | solution.py:211
  116.2 2.0 %collective-permute-start.32 = (bf16[64,1280]{1,0:T(8,128)(2,1)S(1)}, bf16[64,1280]{1,0:T(8,128)(2,1)S(1)}, u32[]{:S(2)}, u32[]{:S(2)}) collective-permute-start(bf16[64,1280]{1,0:T(8,128)(2,1)S(1)} %collective-permute-done.30.refs_1_), channel_id=1, source_target_pairs={{0,3},{1,62},{2,1},{3,4},{4,7},{5,2},{6,5},{7,8},{8,11},{9,6},{10,... | collective-permute-start | bytes 491528 | tf_op jit(solution)/shard_map/ppermute | solution.py:212
  130.1 3.3 %shard_map.88.refs_4_ = f32[384,1280]{1,0:T(8,128)S(1)} custom-call(s32[3]{0:T(128)S(1)} %pad_add_fusion.refs_0_, bf16[384,8192]{1,0:T(8,128)(2,1)} %collective-permute-done.39.refs_1_, bf16[256,1280]{1,0:T(8,128)(2,1)S(1)} %shard_map.81.refs_2_, bf16[256,1280]{1,0:T(8,128)(2,1)S(1)} %copy-done.3, bf16[128,1280]{1,0:T(8,128)(2,1)S(1)} %copy-done.5), custom_call_target="tpu_custom_call" | custom-call | flops 629145600 | bytes 6062080 | tf_op jit(solution)/shard_map/pallas_call | solution.py:125
  133.5 3.6 %shard_map.89.refs_4_ = f32[384,1280]{1,0:T(8,128)S(1)} custom-call(s32[3]{0:T(128)S(1)} %pad_add_fusion.refs_0_, bf16[384,8192]{1,0:T(8,128)(2,1)} %collective-permute-done.39.refs_1_, bf16[384,1280]{1,0:T(8,128)(2,1)S(1)} %shard_map.80.refs_2_, bf16[384,1280]{1,0:T(8,128)(2,1)S(1)} %copy-done.1, ...), custom_call_target="tpu_custom_call", output_to_operand_aliasing={{}: (4, {})} | custom-call | flops 754974720 | bytes 6488064 | tf_op jit(solution)/shard_map/pallas_call | solution.py:125
  137.1 4.5 %shard_map.90.refs_6_ = f32[384,1280]{1,0:T(8,128)S(1)} custom-call(s32[3]{0:T(128)S(1)} %pad_add_fusion.refs_0_, bf16[384,8192]{1,0:T(8,128)(2,1)} %collective-permute-done.39.refs_1_, bf16[384,1280]{1,0:T(8,128)(2,1)S(1)} %shard_map.79.refs_2_, bf16[384,1280]{1,0:T(8,128)(2,1)} %collective-permute-done.36.refs_3_, ...), custom_call_target="tpu_custom_call", output_to_operand_aliasing={{}: (4, {})} | custom-call | flops 754974720 | bytes 6488064 | tf_op jit(solution)/shard_map/pallas_call | solution.py:125
  141.6 4.8 %shard_map.91.refs_6_ = f32[384,1280]{1,0:T(8,128)S(1)} custom-call(s32[3]{0:T(128)S(1)} %pad_add_fusion.refs_0_, bf16[384,8192]{1,0:T(8,128)(2,1)} %collective-permute-done.39.refs_1_, bf16[256,1280]{1,0:T(8,128)(2,1)S(1)} %shard_map.77.refs_2_, bf16[256,1280]{1,0:T(8,128)(2,1)} %collective-permute-done.34.refs_3_, ...), custom_call_target="tpu_custom_call", output_to_operand_aliasing={{}: (6, {})} | custom-call | flops 1006632960 | bytes 7340032 | tf_op jit(solution)/shard_map/pallas_call | solution.py:125
  147.7 3.2 %shard_map.92 = f32[384,1280]{1,0:T(8,128)S(1)} custom-call(s32[3]{0:T(128)S(1)} %pad_add_fusion.refs_0_, bf16[384,896]{1,0:T(8,128)(2,1)S(1)} %shard_map.87.refs_1_, bf16[256,1280]{1,0:T(8,128)(2,1)} %shard_map.74.refs_2_, bf16[256,1280]{1,0:T(8,128)(2,1)} %collective-permute-done.28.refs_3_, ...), custom_call_target="tpu_custom_call", output_to_operand_aliasing={{}: (6, {})} | custom-call | flops 880803840 | bytes 6914048 | tf_op jit(solution)/shard_map/pallas_call | solution.py:125
  151.1 2.4 %shard_map.82.refs_4_ = f32[384,1280]{1,0:T(8,128)S(1)} custom-call(s32[3]{0:T(128)S(1)} %pad_add_fusion.refs_0_, bf16[384,8192]{1,0:T(8,128)(2,1)S(1)} %bitcast.4, bf16[256,1280]{1,0:T(8,128)(2,1)S(1)} %shard_map.81.refs_2_, bf16[256,1280]{1,0:T(8,128)(2,1)S(1)} %copy-done.3, bf16[128,1280]{1,0:T(8,128)(2,1)S(1)} %copy-done.5), custom_call_target="tpu_custom_call" | custom-call | flops 629145600 | bytes 6062080 | tf_op jit(solution)/shard_map/pallas_call | solution.py:125
  153.5 2.6 %shard_map.83.refs_4_ = f32[384,1280]{1,0:T(8,128)S(1)} custom-call(s32[3]{0:T(128)S(1)} %pad_add_fusion.refs_0_, bf16[384,8192]{1,0:T(8,128)(2,1)S(1)} %bitcast.4, bf16[384,1280]{1,0:T(8,128)(2,1)S(1)} %shard_map.80.refs_2_, bf16[384,1280]{1,0:T(8,128)(2,1)S(1)} %copy-done.1, f32[384,1280]{1,0:T(8,128)S(1)} %shard_map.82.refs_4_), custom_call_target="tpu_custom_call", output_to_operand_aliasing={{}: (4, {})} | custom-call | flops 754974720 | bytes 6488064 | tf_op jit(solution)/shard_map/pallas_call | solution.py:125
  156.1 3.2 %shard_map.84.refs_6_ = f32[384,1280]{1,0:T(8,128)S(1)} custom-call(s32[3]{0:T(128)S(1)} %pad_add_fusion.refs_0_, bf16[384,8192]{1,0:T(8,128)(2,1)S(1)} %bitcast.4, bf16[384,1280]{1,0:T(8,128)(2,1)S(1)} %shard_map.79.refs_2_, bf16[384,1280]{1,0:T(8,128)(2,1)} %collective-permute-done.36.refs_3_, ...), custom_call_target="tpu_custom_call", output_to_operand_aliasing={{}: (4, {})} | custom-call | flops 754974720 | bytes 6488064 | tf_op jit(solution)/shard_map/pallas_call | solution.py:125
  159.4 3.7 %shard_map.85.refs_6_ = f32[384,1280]{1,0:T(8,128)S(1)} custom-call(s32[3]{0:T(128)S(1)} %pad_add_fusion.refs_0_, bf16[384,8192]{1,0:T(8,128)(2,1)S(1)} %bitcast.4, bf16[256,1280]{1,0:T(8,128)(2,1)S(1)} %shard_map.77.refs_2_, bf16[256,1280]{1,0:T(8,128)(2,1)} %collective-permute-done.34.refs_3_, ...), custom_call_target="tpu_custom_call", output_to_operand_aliasing={{}: (6, {})} | custom-call | flops 1006632960 | bytes 7340032 | tf_op jit(solution)/shard_map/pallas_call | solution.py:125
  163.1 3.5 %shard_map.86.acc_ref = f32[384,1280]{1,0:T(8,128)S(1)} custom-call(s32[3]{0:T(128)S(1)} %pad_add_fusion.refs_0_, bf16[384,8192]{1,0:T(8,128)(2,1)S(1)} %bitcast.4, bf16[256,1280]{1,0:T(8,128)(2,1)} %shard_map.74.refs_2_, bf16[256,1280]{1,0:T(8,128)(2,1)} %collective-permute-done.28.refs_3_, ...), custom_call_target="tpu_custom_call", output_to_operand_aliasing={{}: (6, {})} | custom-call | flops 880803840 | bytes 6914048 | tf_op jit(solution)/shard_map/pallas_call | solution.py:125
  (113 shorter events, 45.8 us)
Async XLA Ops:
  0.0 126.0 %collective-permute-start.39 = (bf16[384,8192]{1,0:T(8,128)(2,1)}, bf16[384,8192]{1,0:T(8,128)(2,1)}, u32[]{:S(2)}, u32[]{:S(2)}) collective-permute-start(bf16[384,8192]{1,0:T(8,128)(2,1)} %refs_1_.9), channel_id=1, source_target_pairs={{0,1},{1,0},{2,3},{3,2},{4,5},{5,4},{6,7},{7,6},{8,9},{9,8},{10,11... | collective-permute-start | bytes 18874376 | tf_op jit(solution)/shard_map/ppermute | solution.py:208
  26.8 6.0 %collective-permute-start.13 = (bf16[64,1280]{1,0:T(8,128)(2,1)S(1)}, bf16[64,1280]{1,0:T(8,128)(2,1)S(1)}, u32[]{:S(2)}, u32[]{:S(2)}) collective-permute-start(bf16[64,1280]{1,0:T(8,128)(2,1)S(1)} %get-tuple-element.9), channel_id=1, source_target_pairs={{0,3},{1,62},{2,1},{3,4},{4,7},{5,2},{6,5},{7,8},{8,11},{9,6},{10,... | collective-permute-start | bytes 491528 | tf_op jit(solution)/shard_map/ppermute | solution.py:212
  29.0 6.0 %collective-permute-start.1 = (bf16[64,1280]{1,0:T(8,128)(2,1)S(1)}, bf16[64,1280]{1,0:T(8,128)(2,1)S(1)}, u32[]{:S(2)}, u32[]{:S(2)}) collective-permute-start(bf16[64,1280]{1,0:T(8,128)(2,1)S(1)} %collective-permute-done.refs_0_), channel_id=1, source_target_pairs={{0,3},{1,62},{2,1},{3,4},{4,7},{5,2},{6,5},{7,8},{8,11},{9,6},{10,... | collective-permute-start | bytes 491528 | tf_op jit(solution)/shard_map/ppermute | solution.py:211
  32.7 6.0 %collective-permute-start.14 = (bf16[64,1280]{1,0:T(8,128)(2,1)S(1)}, bf16[64,1280]{1,0:T(8,128)(2,1)S(1)}, u32[]{:S(2)}, u32[]{:S(2)}) collective-permute-start(bf16[64,1280]{1,0:T(8,128)(2,1)S(1)} %collective-permute-done.13.refs_1_), channel_id=1, source_target_pairs={{0,3},{1,62},{2,1},{3,4},{4,7},{5,2},{6,5},{7,8},{8,11},{9,6},{10,... | collective-permute-start | bytes 491528 | tf_op jit(solution)/shard_map/ppermute | solution.py:212
  35.0 6.0 %collective-permute-start.2 = (bf16[64,1280]{1,0:T(8,128)(2,1)S(1)}, bf16[64,1280]{1,0:T(8,128)(2,1)S(1)}, u32[]{:S(2)}, u32[]{:S(2)}) collective-permute-start(bf16[64,1280]{1,0:T(8,128)(2,1)S(1)} %collective-permute-done.1.refs_2_), channel_id=1, source_target_pairs={{0,3},{1,62},{2,1},{3,4},{4,7},{5,2},{6,5},{7,8},{8,11},{9,6},{10,... | collective-permute-start | bytes 491528 | tf_op jit(solution)/shard_map/ppermute | solution.py:211
  38.7 6.0 %collective-permute-start.15 = (bf16[64,1280]{1,0:T(8,128)(2,1)S(1)}, bf16[64,1280]{1,0:T(8,128)(2,1)S(1)}, u32[]{:S(2)}, u32[]{:S(2)}) collective-permute-start(bf16[64,1280]{1,0:T(8,128)(2,1)S(1)} %collective-permute-done.14.refs_3_), channel_id=1, source_target_pairs={{0,3},{1,62},{2,1},{3,4},{4,7},{5,2},{6,5},{7,8},{8,11},{9,6},{10,... | collective-permute-start | bytes 491528 | tf_op jit(solution)/shard_map/ppermute | solution.py:212
  40.9 6.0 %collective-permute-start.3 = (bf16[64,1280]{1,0:T(8,128)(2,1)S(1)}, bf16[64,1280]{1,0:T(8,128)(2,1)S(1)}, u32[]{:S(2)}, u32[]{:S(2)}) collective-permute-start(bf16[64,1280]{1,0:T(8,128)(2,1)S(1)} %collective-permute-done.2.refs_0_), channel_id=1, source_target_pairs={{0,3},{1,62},{2,1},{3,4},{4,7},{5,2},{6,5},{7,8},{8,11},{9,6},{10,... | collective-permute-start | bytes 491528 | tf_op jit(solution)/shard_map/ppermute | solution.py:211
  46.9 6.0 %collective-permute-start.4 = (bf16[64,1280]{1,0:T(8,128)(2,1)S(1)}, bf16[64,1280]{1,0:T(8,128)(2,1)S(1)}, u32[]{:S(2)}, u32[]{:S(2)}) collective-permute-start(bf16[64,1280]{1,0:T(8,128)(2,1)S(1)} %collective-permute-done.3.refs_2_), channel_id=1, source_target_pairs={{0,3},{1,62},{2,1},{3,4},{4,7},{5,2},{6,5},{7,8},{8,11},{9,6},{10,... | collective-permute-start | bytes 491528 | tf_op jit(solution)/shard_map/ppermute | solution.py:211
  50.6 6.0 %collective-permute-start.17 = (bf16[64,1280]{1,0:T(8,128)(2,1)S(1)}, bf16[64,1280]{1,0:T(8,128)(2,1)S(1)}, u32[]{:S(2)}, u32[]{:S(2)}) collective-permute-start(bf16[64,1280]{1,0:T(8,128)(2,1)S(1)} %collective-permute-done.16.refs_3_), channel_id=1, source_target_pairs={{0,3},{1,62},{2,1},{3,4},{4,7},{5,2},{6,5},{7,8},{8,11},{9,6},{10,... | collective-permute-start | bytes 491528 | tf_op jit(solution)/shard_map/ppermute | solution.py:212
  52.9 6.0 %collective-permute-start.5 = (bf16[64,1280]{1,0:T(8,128)(2,1)S(1)}, bf16[64,1280]{1,0:T(8,128)(2,1)S(1)}, u32[]{:S(2)}, u32[]{:S(2)}) collective-permute-start(bf16[64,1280]{1,0:T(8,128)(2,1)S(1)} %collective-permute-done.4.refs_4_), channel_id=1, source_target_pairs={{0,3},{1,62},{2,1},{3,4},{4,7},{5,2},{6,5},{7,8},{8,11},{9,6},{10,... | collective-permute-start | bytes 491528 | tf_op jit(solution)/shard_map/ppermute | solution.py:211
  56.6 6.0 %collective-permute-start.18 = (bf16[64,1280]{1,0:T(8,128)(2,1)S(1)}, bf16[64,1280]{1,0:T(8,128)(2,1)S(1)}, u32[]{:S(2)}, u32[]{:S(2)}) collective-permute-start(bf16[64,1280]{1,0:T(8,128)(2,1)S(1)} %collective-permute-done.17.refs_5_), channel_id=1, source_target_pairs={{0,3},{1,62},{2,1},{3,4},{4,7},{5,2},{6,5},{7,8},{8,11},{9,6},{10,... | collective-permute-start | bytes 491528 | tf_op jit(solution)/shard_map/ppermute | solution.py:212
  58.8 6.0 %collective-permute-start.6 = (bf16[64,1280]{1,0:T(8,128)(2,1)S(1)}, bf16[64,1280]{1,0:T(8,128)(2,1)S(1)}, u32[]{:S(2)}, u32[]{:S(2)}) collective-permute-start(bf16[64,1280]{1,0:T(8,128)(2,1)S(1)} %collective-permute-done.5.refs_0_), channel_id=1, source_target_pairs={{0,3},{1,62},{2,1},{3,4},{4,7},{5,2},{6,5},{7,8},{8,11},{9,6},{10,... | collective-permute-start | bytes 491528 | tf_op jit(solution)/shard_map/ppermute | solution.py:211
  62.5 6.0 %collective-permute-start.19 = (bf16[64,1280]{1,0:T(8,128)(2,1)S(1)}, bf16[64,1280]{1,0:T(8,128)(2,1)S(1)}, u32[]{:S(2)}, u32[]{:S(2)}) collective-permute-start(bf16[64,1280]{1,0:T(8,128)(2,1)S(1)} %collective-permute-done.18.refs_1_), channel_id=1, source_target_pairs={{0,3},{1,62},{2,1},{3,4},{4,7},{5,2},{6,5},{7,8},{8,11},{9,6},{10,... | collective-permute-start | bytes 491528 | tf_op jit(solution)/shard_map/ppermute | solution.py:212
  64.8 6.0 %collective-permute-start.7 = (bf16[64,1280]{1,0:T(8,128)(2,1)S(1)}, bf16[64,1280]{1,0:T(8,128)(2,1)S(1)}, u32[]{:S(2)}, u32[]{:S(2)}) collective-permute-start(bf16[64,1280]{1,0:T(8,128)(2,1)S(1)} %collective-permute-done.6.refs_2_), channel_id=1, source_target_pairs={{0,3},{1,62},{2,1},{3,4},{4,7},{5,2},{6,5},{7,8},{8,11},{9,6},{10,... | collective-permute-start | bytes 491528 | tf_op jit(solution)/shard_map/ppermute | solution.py:211
  68.5 6.0 %collective-permute-start.20 = (bf16[64,1280]{1,0:T(8,128)(2,1)S(1)}, bf16[64,1280]{1,0:T(8,128)(2,1)S(1)}, u32[]{:S(2)}, u32[]{:S(2)}) collective-permute-start(bf16[64,1280]{1,0:T(8,128)(2,1)S(1)} %collective-permute-done.19.refs_3_), channel_id=1, source_target_pairs={{0,3},{1,62},{2,1},{3,4},{4,7},{5,2},{6,5},{7,8},{8,11},{9,6},{10,... | collective-permute-start | bytes 491528 | tf_op jit(solution)/shard_map/ppermute | solution.py:212
  70.7 6.0 %collective-permute-start.8 = (bf16[64,1280]{1,0:T(8,128)(2,1)S(1)}, bf16[64,1280]{1,0:T(8,128)(2,1)S(1)}, u32[]{:S(2)}, u32[]{:S(2)}) collective-permute-start(bf16[64,1280]{1,0:T(8,128)(2,1)S(1)} %collective-permute-done.7.refs_4_), channel_id=1, source_target_pairs={{0,3},{1,62},{2,1},{3,4},{4,7},{5,2},{6,5},{7,8},{8,11},{9,6},{10,... | collective-permute-start | bytes 491528 | tf_op jit(solution)/shard_map/ppermute | solution.py:211
  74.4 8.0 %collective-permute-start.21 = (bf16[64,1280]{1,0:T(8,128)(2,1)S(1)}, bf16[64,1280]{1,0:T(8,128)(2,1)S(1)}, u32[]{:S(2)}, u32[]{:S(2)}) collective-permute-start(bf16[64,1280]{1,0:T(8,128)(2,1)S(1)} %collective-permute-done.20.refs_5_), channel_id=1, source_target_pairs={{0,3},{1,62},{2,1},{3,4},{4,7},{5,2},{6,5},{7,8},{8,11},{9,6},{10,... | collective-permute-start | bytes 491528 | tf_op jit(solution)/shard_map/ppermute | solution.py:212
  80.4 23.8 %collective-permute-start.38 = (bf16[256,1280]{1,0:T(8,128)(2,1)S(1)}, bf16[256,1280]{1,0:T(8,128)(2,1)S(1)}, u32[]{:S(2)}, u32[]{:S(2)}) collective-permute-start(bf16[256,1280]{1,0:T(8,128)(2,1)S(1)} %shard_map.81.refs_2_), channel_id=1, source_target_pairs={{0,129},{1,64},{2,67},{3,130},{4,133},{5,68},{6,71},{7,134},{8,137... | collective-permute-start | bytes 1966088 | tf_op jit(solution)/shard_map/ppermute | solution.py:220
  82.4 6.0 %collective-permute-start.22 = (bf16[64,1280]{1,0:T(8,128)(2,1)S(1)}, bf16[64,1280]{1,0:T(8,128)(2,1)S(1)}, u32[]{:S(2)}, u32[]{:S(2)}) collective-permute-start(bf16[64,1280]{1,0:T(8,128)(2,1)S(1)} %collective-permute-done.21.refs_1_), channel_id=1, source_target_pairs={{0,3},{1,62},{2,1},{3,4},{4,7},{5,2},{6,5},{7,8},{8,11},{9,6},{10,... | collective-permute-start | bytes 491528 | tf_op jit(solution)/shard_map/ppermute | solution.py:212
  82.6 6.6 %collective-permute-start.10 = (bf16[64,1280]{1,0:T(8,128)(2,1)S(1)}, bf16[64,1280]{1,0:T(8,128)(2,1)S(1)}, u32[]{:S(2)}, u32[]{:S(2)}) collective-permute-start(bf16[64,1280]{1,0:T(8,128)(2,1)S(1)} %collective-permute-done.9.refs_2_), channel_id=1, source_target_pairs={{0,3},{1,62},{2,1},{3,4},{4,7},{5,2},{6,5},{7,8},{8,11},{9,6},{10,... | collective-permute-start | bytes 491528 | tf_op jit(solution)/shard_map/ppermute | solution.py:211
  86.4 32.8 %collective-permute-start.37 = (bf16[384,1280]{1,0:T(8,128)(2,1)S(1)}, bf16[384,1280]{1,0:T(8,128)(2,1)S(1)}, u32[]{:S(2)}, u32[]{:S(2)}) collective-permute-start(bf16[384,1280]{1,0:T(8,128)(2,1)S(1)} %shard_map.80.refs_2_), channel_id=1, source_target_pairs={{0,129},{1,64},{2,67},{3,130},{4,133},{5,68},{6,71},{7,134},{8,137... | collective-permute-start | bytes 2949128 | tf_op jit(solution)/shard_map/ppermute | solution.py:220
  89.2 6.0 %collective-permute-start.11 = (bf16[64,1280]{1,0:T(8,128)(2,1)S(1)}, bf16[64,1280]{1,0:T(8,128)(2,1)S(1)}, u32[]{:S(2)}, u32[]{:S(2)}) collective-permute-start(bf16[64,1280]{1,0:T(8,128)(2,1)S(1)} %collective-permute-done.10.refs_0_), channel_id=1, source_target_pairs={{0,3},{1,62},{2,1},{3,4},{4,7},{5,2},{6,5},{7,8},{8,11},{9,6},{10,... | collective-permute-start | bytes 491528 | tf_op jit(solution)/shard_map/ppermute | solution.py:211
  98.2 8.1 %collective-permute-start.25 = (bf16[64,1280]{1,0:T(8,128)(2,1)S(1)}, bf16[64,1280]{1,0:T(8,128)(2,1)S(1)}, u32[]{:S(2)}, u32[]{:S(2)}) collective-permute-start(bf16[64,1280]{1,0:T(8,128)(2,1)S(1)} %collective-permute-done.24.refs_3_), channel_id=1, source_target_pairs={{0,3},{1,62},{2,1},{3,4},{4,7},{5,2},{6,5},{7,8},{8,11},{9,6},{10,... | collective-permute-start | bytes 491528 | tf_op jit(solution)/shard_map/ppermute | solution.py:212
  104.3 32.8 %collective-permute-start.36 = (bf16[384,1280]{1,0:T(8,128)(2,1)S(1)}, bf16[384,1280]{1,0:T(8,128)(2,1)}, u32[]{:S(2)}, u32[]{:S(2)}) collective-permute-start(bf16[384,1280]{1,0:T(8,128)(2,1)S(1)} %shard_map.79.refs_2_), channel_id=1, source_target_pairs={{0,129},{1,64},{2,67},{3,130},{4,133},{5,68},{6,71},{7,134},{8,137... | collective-permute-start | bytes 2949128 | tf_op jit(solution)/shard_map/ppermute | solution.py:220
  106.5 6.8 %collective-permute-start.29 = (bf16[64,1280]{1,0:T(8,128)(2,1)S(1)}, bf16[64,1280]{1,0:T(8,128)(2,1)S(1)}, u32[]{:S(2)}, u32[]{:S(2)}) collective-permute-start(bf16[64,1280]{1,0:T(8,128)(2,1)S(1)} %collective-permute-done.26.refs_2_), channel_id=1, source_target_pairs={{0,3},{1,62},{2,1},{3,4},{4,7},{5,2},{6,5},{7,8},{8,11},{9,6},{10,... | collective-permute-start | bytes 491528 | tf_op jit(solution)/shard_map/ppermute | solution.py:211
  113.2 8.5 %collective-permute-start.31 = (bf16[64,1280]{1,0:T(8,128)(2,1)S(1)}, bf16[64,1280]{1,0:T(8,128)(2,1)S(1)}, u32[]{:S(2)}, u32[]{:S(2)}) collective-permute-start(bf16[64,1280]{1,0:T(8,128)(2,1)S(1)} %collective-permute-done.29.refs_0_), channel_id=1, source_target_pairs={{0,3},{1,62},{2,1},{3,4},{4,7},{5,2},{6,5},{7,8},{8,11},{9,6},{10,... | collective-permute-start | bytes 491528 | tf_op jit(solution)/shard_map/ppermute | solution.py:211
  116.2 6.6 %collective-permute-start.32 = (bf16[64,1280]{1,0:T(8,128)(2,1)S(1)}, bf16[64,1280]{1,0:T(8,128)(2,1)S(1)}, u32[]{:S(2)}, u32[]{:S(2)}) collective-permute-start(bf16[64,1280]{1,0:T(8,128)(2,1)S(1)} %collective-permute-done.30.refs_1_), channel_id=1, source_target_pairs={{0,3},{1,62},{2,1},{3,4},{4,7},{5,2},{6,5},{7,8},{8,11},{9,6},{10,... | collective-permute-start | bytes 491528 | tf_op jit(solution)/shard_map/ppermute | solution.py:212
  120.2 21.4 %collective-permute-start.34 = (bf16[256,1280]{1,0:T(8,128)(2,1)S(1)}, bf16[256,1280]{1,0:T(8,128)(2,1)}, u32[]{:S(2)}, u32[]{:S(2)}) collective-permute-start(bf16[256,1280]{1,0:T(8,128)(2,1)S(1)} %shard_map.77.refs_2_), channel_id=1, source_target_pairs={{0,129},{1,64},{2,67},{3,130},{4,133},{5,68},{6,71},{7,134},{8,137... | collective-permute-start | bytes 1966088 | tf_op jit(solution)/shard_map/ppermute | solution.py:220
  121.7 19.9 %collective-permute-start.35 = (bf16[256,1280]{1,0:T(8,128)(2,1)}, bf16[256,1280]{1,0:T(8,128)(2,1)}, u32[]{:S(2)}, u32[]{:S(2)}) collective-permute-start(bf16[256,1280]{1,0:T(8,128)(2,1)} %shard_map.78.refs_4_), channel_id=1, source_target_pairs={{0,129},{1,64},{2,67},{3,130},{4,133},{5,68},{6,71},{7,134},{8,137... | collective-permute-start | bytes 1966088 | tf_op jit(solution)/shard_map/ppermute | solution.py:220
  123.5 24.3 %collective-permute-start.28 = (bf16[256,1280]{1,0:T(8,128)(2,1)}, bf16[256,1280]{1,0:T(8,128)(2,1)}, u32[]{:S(2)}, u32[]{:S(2)}) collective-permute-start(bf16[256,1280]{1,0:T(8,128)(2,1)} %shard_map.74.refs_2_), channel_id=1, source_target_pairs={{0,129},{1,64},{2,67},{3,130},{4,133},{5,68},{6,71},{7,134},{8,137... | collective-permute-start | bytes 1966088 | tf_op jit(solution)/shard_map/ppermute | solution.py:220
  126.0 21.8 %collective-permute-start.33 = (bf16[128,1280]{1,0:T(8,128)(2,1)S(1)}, bf16[128,1280]{1,0:T(8,128)(2,1)S(1)}, u32[]{:S(2)}, u32[]{:S(2)}) collective-permute-start(bf16[128,1280]{1,0:T(8,128)(2,1)S(1)} %shard_map.76), channel_id=1, source_target_pairs={{0,129},{1,64},{2,67},{3,130},{4,133},{5,68},{6,71},{7,134},{8,137... | collective-permute-start | bytes 983048 | tf_op jit(solution)/shard_map/ppermute | solution.py:220
  150.9 15.7 %collective-permute-start.40 = (f32[384,1280]{1,0:T(8,128)S(1)}, f32[384,1280]{1,0:T(8,128)S(1)}, u32[]{:S(2)}, u32[]{:S(2)}) collective-permute-start(f32[384,1280]{1,0:T(8,128)S(1)} %shard_map.92), channel_id=1, source_target_pairs={{0,1},{1,0},{2,3},{3,2},{4,5},{5,4},{6,7},{7,6},{8,9},{9,8},{10,11... | collective-permute-start | bytes 5898248 | tf_op jit(solution)/shard_map/ppermute | solution.py:234
  (29 other events, 127.0 us)
